TPU v7x, 32 devices: a whole 2x2x4 slice. The times are simulated.
32 devices in a mesh: head: 2 (over x), ctx: 16 (over z, y, core).
Axes of the slice: x: 2, y: 2, z: 4, core: 2. Of those that a mesh axis runs over, the one named last changes fastest.
Arguments:
- queries: bfloat16 [8192, 5120], P(('head', 'ctx')), may hold values from -6 to 6
- keys: bfloat16 [8192, 5120], P(('head', 'ctx')), may hold values from -6 to 6
- values: bfloat16 [8192, 5120], P(('head', 'ctx')), may hold values from -6 to 6
- rates: bfloat16 [8192, 8], P(('head', 'ctx')), may hold values from 0.099609375 to 1
- q_gain: float32 [5120], replicated, may hold values from 0.1 to 1.9
- k_gain: float32 [5120], replicated, may hold values from 0.2 to 4.5, as said below
- w_first: float32 [8, 640, 640], P('head'), may hold values from -0.2766993 to 0.2766993
- w_second: float32 [8, 640, 640], P('head'), may hold values from -0.25 to 0.25
- w_third: float32 [8, 640, 640], P('head'), may hold values from -0.2766993 to 0.2766993
Outputs:
- attended: bfloat16 [8192, 5120], P(('head', 'ctx'))
Inputs may be any that keep to these rules, and one draw needn't show every extreme that they name: `k_gain`: positive per-feature gains.
All inputs are finite; a program needn't handle non-finite values.
Results may differ from a plain program's by a relative error of at most 0.015.
Values may be sent and summed in bfloat16 or wider, within the bound.
No kernel may reach another device: no remote copies, remote signals or barrier semaphores. Data moves between devices by JAX's collectives and lax.ppermute only.
A program may use at most 128 MiB of HBM per device.

v0:
```python
import jax
import jax.numpy as jnp
from jax import lax
from jax.sharding import PartitionSpec as P

NS_STEPS = 2


epsilon = 1e-06
frob_eps = 1e-07
coeff_a = 3.4445
coeff_b = -4.775
coeff_c = 2.0315
step_size = 1.0


def rms_scale(inputs, gain):
    widened = inputs.astype(jnp.float32)
    factor = lax.rsqrt(jnp.mean(widened * widened, axis=-1, keepdims=True) + epsilon)
    return (widened * factor * gain).astype(jnp.bfloat16)


def update_rows(own_rows, square_rows, full_square, full_iterate):
    polynomial = (
        coeff_b * square_rows.astype(jnp.float32)
        + coeff_c
        * jnp.einsum("hij,hjk->hik", square_rows, full_square, preferred_element_type=jnp.float32)
    ).astype(jnp.bfloat16)
    return (
        coeff_a * own_rows.astype(jnp.float32)
        + jnp.einsum("hij,hjk->hik", polynomial, full_iterate, preferred_element_type=jnp.float32)
    ).astype(jnp.bfloat16)


def orthogonal(gradient):
    frob_total = jnp.sqrt(jnp.sum(gradient * gradient, axis=(1, 2), keepdims=True))
    iterate = (gradient / (frob_total + frob_eps)).astype(jnp.bfloat16)
    for repeat_index in range(NS_STEPS):
        square = jnp.einsum(
            "hij,hkj->hik", iterate, iterate, preferred_element_type=jnp.float32
        ).astype(jnp.bfloat16)
        iterate = update_rows(iterate, square, square, iterate)
    return iterate


def per_device(queries, keys, values, rates, q_gain, k_gain, w_first, w_second, w_third):
    queries_n = rms_scale(queries, q_gain)
    keys_n = rms_scale(keys, k_gain)
    arrived = (
        lax.all_to_all(queries_n, "head", split_axis=1, concat_axis=0, tiled=True),
        lax.all_to_all(keys_n, "head", split_axis=1, concat_axis=0, tiled=True),
        lax.all_to_all(values, "head", split_axis=1, concat_axis=0, tiled=True),
        lax.all_to_all(rates, "head", split_axis=1, concat_axis=0, tiled=True),
    )
    heads_here = w_first.shape[0]
    width = w_first.shape[1]
    token_rows = arrived[0].shape[0]
    query_local = arrived[0].reshape(token_rows, heads_here, width)
    key_local = arrived[1].reshape(token_rows, heads_here, width)
    value_local = arrived[2].reshape(token_rows, heads_here, width)
    rate_local = arrived[3]
    first_b = w_first.astype(jnp.bfloat16)
    second_b = w_second.astype(jnp.bfloat16)
    third_b = w_third.astype(jnp.bfloat16)
    pre_first = jnp.einsum("thd,hde->the", key_local, first_b, preferred_element_type=jnp.float32)
    pre_third = jnp.einsum("thd,hde->the", key_local, third_b, preferred_element_type=jnp.float32)
    sigmoid = jax.nn.sigmoid(pre_first)
    activ = pre_first * sigmoid
    hidden = (activ * pre_third).astype(jnp.bfloat16)
    scaled_v = (
        rate_local[:, :, None].astype(jnp.float32) * value_local.astype(jnp.float32)
    ).astype(jnp.bfloat16)
    back_hidden = jnp.einsum("the,hde->thd", scaled_v, second_b, preferred_element_type=jnp.float32)
    grad_pre_first = (
        back_hidden * pre_third * sigmoid * (1.0 + pre_first * (1.0 - sigmoid))
    ).astype(jnp.bfloat16)
    grad_pre_third = (back_hidden * activ).astype(jnp.bfloat16)
    grad_first = jnp.einsum(
        "thd,the->hde", key_local, grad_pre_first, preferred_element_type=jnp.float32
    )
    grad_second = jnp.einsum("thd,the->hde", hidden, scaled_v, preferred_element_type=jnp.float32)
    grad_third = jnp.einsum(
        "thd,the->hde", key_local, grad_pre_third, preferred_element_type=jnp.float32
    )
    full_first, full_second, full_third = lax.psum((grad_first, grad_second, grad_third), "ctx")
    new_first = (w_first + step_size * orthogonal(full_first).astype(jnp.float32)).astype(
        jnp.bfloat16
    )
    new_second = (w_second + step_size * orthogonal(full_second).astype(jnp.float32)).astype(
        jnp.bfloat16
    )
    new_third = (w_third + step_size * orthogonal(full_third).astype(jnp.float32)).astype(
        jnp.bfloat16
    )
    query_first = jnp.einsum(
        "thd,hde->the", query_local, new_first, preferred_element_type=jnp.float32
    )
    query_third = jnp.einsum(
        "thd,hde->the", query_local, new_third, preferred_element_type=jnp.float32
    )
    gated = (jax.nn.silu(query_first) * query_third).astype(jnp.bfloat16)
    result = jnp.einsum("thd,hde->the", gated, new_second, preferred_element_type=jnp.float32)
    normed = (
        result * lax.rsqrt(jnp.mean(result * result, axis=-1, keepdims=True) + epsilon)
    ).astype(jnp.bfloat16)
    return lax.all_to_all(
        normed.reshape(token_rows, heads_here * width),
        "head",
        split_axis=0,
        concat_axis=1,
        tiled=True,
    )


def solution(mesh):
    return jax.shard_map(
        per_device,
        mesh=mesh,
        in_specs=(
            P(("head", "ctx"), None),
            P(("head", "ctx"), None),
            P(("head", "ctx"), None),
            P(("head", "ctx"), None),
            P(),
            P(),
            P("head", None, None),
            P("head", None, None),
            P("head", None, None),
        ),
        out_specs=P(("head", "ctx"), None),
        check_vma=False,
    )
```

profile of v0, /device:TPU:0, one launch (start us, length us, event | category | flops | bytes accessed | tf_op | source)
XLA Modules:
  0.0 686.7 jit_solution(3573755864242421686)
XLA Ops:
  7.8 4.2 all-to-all-start.1
  25.9 27.5 %all-to-all-done = bf16[256,2,2560]{2,0,1:T(8,128)(2,1)S(1)} async-done(((bf16[256,2,2560]{2,0,1:T(8,128)(2,1)}), bf16[256,2,2560]{2,0,1:T(8,128)(2,1)S(1)}, u32[]{:S(2)}, u32[]{:S(2)}) %all-to-all-start) | async-done | bytes 2621472 | tf_op jit(solution)/shard_map/all_to_all | solution.py:51
  53.4 5.0 all-to-all-start.2
  60.9 4.0 copy.41
  64.8 23.8 %all-to-all-done.2 = bf16[256,2,2560]{2,0,1:T(8,128)(2,1)} async-done(((bf16[256,2,2560]{2,0,1:T(8,128)(2,1)}), bf16[256,2,2560]{2,0,1:T(8,128)(2,1)}, u32[]{:S(2)}, u32[]{:S(2)}) %all-to-all-start.2) | async-done | bytes 2621472 | tf_op jit(solution)/shard_map/all_to_all | solution.py:52
  88.6 4.7 convert_bitcast_fusion
  93.3 7.3 %reshape.86 = f32[512,4,640]{2,1,0:T(4,128)} reshape(f32[2,256,2560]{2,1,0:T(8,128)} %convert_bitcast_fusion) | data formatting | bytes 10485760 | tf_op jit(solution)/shard_map/convert_element_type | solution.py:71
  100.6 5.0 fusion.47
  105.6 7.3 %fusion.49 = f32[4,512,640]{2,1,0:T(8,128)} fusion(bf16[512,4,640]{0,2,1:T(8,128)(2,1)S(1)} %copy.41, f32[4,640,640]{2,1,0:T(8,128)} %param.15), kind=kOutput, calls=%fused_computation.87 | convolution fusion | flops 1679360000 | bytes 14417920 | tf_op jit(solution)/shard_map/thd,hde->the/dot_general | solution.py:65
  114.1 4.5 fusion.30
  118.6 8.1 %fusion.51 = f32[4,640,640]{2,1,0:T(8,128)} fusion(f32[4,512,640]{2,1,0:T(8,128)S(1)} %fusion.47, bf16[512,4,640]{2,1,0:T(4,128)(2,1)S(1)} %multiply_convert_fusion, f32[4,512,640]{2,1,0:T(8,128)} %fusion.49), kind=kOutput, calls=%fused_computation.89 | convolution fusion | flops 1685585920 | bytes 19660800 | tf_op jit(solution)/shard_map/thd,the->hde/dot_general | solution.py:81
  126.7 7.6 %fusion.53 = f32[4,640,640]{2,1,0:T(8,128)} fusion(bf16[512,4,640]{0,2,1:T(8,128)(2,1)S(1)} %copy.41, f32[4,512,640]{2,1,0:T(8,128)S(1)} %copy-done.3, f32[4,512,640]{2,1,0:T(8,128)} %fusion.49), kind=kOutput, calls=%fused_computation.90 | convolution fusion | flops 1685585920 | bytes 19660800 | tf_op jit(solution)/shard_map/thd,the->hde/dot_general | solution.py:82
  134.3 7.8 %fusion.56 = f32[4,640,640]{2,1,0:T(8,128)} fusion(bf16[512,4,640]{0,2,1:T(8,128)(2,1)S(1)} %copy.41, f32[4,512,640]{2,1,0:T(8,128)S(1)} %copy-done.3, f32[4,512,640]{2,1,0:T(8,128)S(1)} %fusion.47, f32[4,512,640]{2,1,0:T(8,128)} %fusion.49), kind=kOutput, calls=%fused_computation.94 | convolution fusion | flops 1690828800 | bytes 24903680 | tf_op jit(solution)/shard_map/thd,the->hde/dot_general | solution.py:78
  145.4 32.2 %all_to_all.77 = bf16[256,2,2560]{2,0,1:T(8,128)(2,1)S(1)} all-to-all(bf16[256,2,2560]{2,0,1:T(8,128)(2,1)S(1)} %bitcast.133), channel_id=1, replica_groups=mesh['head'=2,'ctx'=16] {'head'}, dimensions={1} | all-to-all | bytes 5242880 | tf_op jit(solution)/shard_map/all_to_all | solution.py:50
  179.8 303.8 %all-reduce.3.cloned.1.call-done = (f32[4,640,640]{2,1,0:T(8,128)}, f32[4,640,640]{2,1,0:T(8,128)}, f32[4,640,640]{2,1,0:T(8,128)}) async-done(((f32[4,640,640]{2,1,0:T(8,128)}, f32[4,640,640]{2,1,0:T(8,128)}, f32[4,640,640]{2,1,0:T(8,128)}), (f32[4,640,640]{2,1,0:T(8,128)}, f32[4,640,640]{2,1,0:T(8,128)}, f32[4,640,640]{2,1,0:T(8,128)})) %all-reduce.3.cloned.1.call-update) | async-done | bytes 19660816 | tf_op jit(solution)/shard_map/psum | solution.py:85
  483.6 5.9 multiply_reduce_fusion
  490.2 4.7 convolution_convert_fusion.1
  494.9 15.1 %add_convert_fusion.3 = bf16[4,640,640]{2,1,0:T(8,128)(2,1)} fusion(bf16[4,640,640]{2,1,0:T(8,128)(2,1)} %convolution_convert_fusion.1, f32[4,640,640]{2,1,0:T(8,128)} %get-tuple-element.6, f32[4]{0:T(128)S(1)} %sqrt_add_fusion), kind=kOutput, calls=%fused_computation.3 | convolution fusion | flops 4215603200 | bytes 13107216 | tf_op jit(solution)/shard_map/hij,hjk->hik/dot_general | solution.py:31
  510.1 6.2 convolution_convert_fusion
  516.3 5.0 fusion.95
  521.3 4.7 convolution_convert_fusion.3
  526.0 15.6 %add_convert_fusion.8 = bf16[4,640,640]{2,1,0:T(8,128)(2,1)} fusion(bf16[4,640,640]{2,1,0:T(8,128)(2,1)} %convolution_convert_fusion.3, f32[4,640,640]{2,1,0:T(8,128)} %get-tuple-element.7, f32[4]{0:T(128)S(1)} %sqrt_add_fusion.1), kind=kOutput, calls=%fused_computation.10 | convolution fusion | flops 4215603200 | bytes 13107216 | tf_op jit(solution)/shard_map/hij,hjk->hik/dot_general | solution.py:31
  541.6 6.1 convolution_convert_fusion.2
  549.4 5.0 fusion.94
  554.3 15.2 %fusion.29 = f32[4,640,512]{1,2,0:T(8,128)} fusion(f32[4,640,640]{2,1,0:T(8,128)} %param.17, bf16[4,640,640]{2,1,0:T(8,128)(2,1)} %add_convert_fusion.3, bf16[512,4,640]{2,1,0:T(4,128)(2,1)} %reshape.84, f32[4,640,640]{2,1,0:T(8,128)} %fusion.95, bf16[4,640,640]{2,1,0:T(8,128)(2,1)S(1)} %convolution_convert_fusion), kind=kOutput, calls=%fused_computation.67 | convolution fusion | flops 3794534400 | bytes 27525120 | tf_op jit(solution)/shard_map/thd,hde->the/dot_general | solution.py:98
  569.5 16.2 %fusion.26 = f32[4,640,512]{1,2,0:T(8,128)} fusion(f32[4,640,640]{2,1,0:T(8,128)} %param.15, bf16[4,640,640]{2,1,0:T(8,128)(2,1)} %add_convert_fusion.8, bf16[512,4,640]{2,1,0:T(4,128)(2,1)} %reshape.84, f32[4,640,640]{2,1,0:T(8,128)} %fusion.94, bf16[4,640,640]{2,1,0:T(8,128)(2,1)} %copy-done), kind=kOutput, calls=%fused_computation.64 | convolution fusion | flops 3794534400 | bytes 27525120 | tf_op jit(solution)/shard_map/thd,hde->the/dot_general | solution.py:95
  589.2 8.2 %convolution_convert_fusion.5 = bf16[4,640,640]{2,1,0:T(8,128)(2,1)S(1)} fusion(f32[4,640,640]{2,1,0:T(8,128)} %get-tuple-element.5, f32[4]{0:T(128)S(1)} %sqrt_add_fusion.2), kind=kOutput, calls=%fused_computation.100 | convolution fusion | flops 2102067200 | bytes 9830416 | tf_op jit(solution)/shard_map/hij,hkj->hik/dot_general | solution.py:39
  597.4 12.1 %add_convert_fusion.13 = bf16[4,640,640]{2,1,0:T(8,128)(2,1)} fusion(bf16[4,640,640]{2,1,0:T(8,128)(2,1)S(1)} %convolution_convert_fusion.5, f32[4,640,640]{2,1,0:T(8,128)} %get-tuple-element.5, f32[4]{0:T(128)S(1)} %sqrt_add_fusion.2), kind=kOutput, calls=%fused_computation.17 | convolution fusion | flops 4215603200 | bytes 13107216 | tf_op jit(solution)/shard_map/hij,hjk->hik/dot_general | solution.py:31
  609.5 6.2 convolution_convert_fusion.4
  615.7 5.0 fusion.93
  620.6 14.9 %fusion.6 = (f32[512,4]{0,1:T(4,128)S(1)}, f32[4,640,512]{2,1,0:T(8,128)}) fusion(f32[4,640,512]{1,2,0:T(8,128)} %fusion.29, f32[4,640,512]{1,2,0:T(8,128)} %fusion.26, f32[4,640,640]{2,1,0:T(8,128)} %param.16, bf16[4,640,640]{2,1,0:T(8,128)(2,1)} %add_convert_fusion.13, f32[4,640,640]{2,1,0:T(8,128)} %fusion.93, ...), kind=kOutput, calls=%fused_computation.33 | convolution fusion | flops 3805018112 | bytes 35397632 | tf_op jit(solution)/shard_map/thd,hde->the/dot_general | solution.py:102
  643.6 33.0 %all_to_all.78 = bf16[2,256,2560]{1,2,0:T(8,128)(2,1)S(1)} all-to-all(bf16[2,256,2560]{1,2,0:T(8,128)(2,1)S(1)} %copy.51), channel_id=1, replica_groups=mesh['head'=2,'ctx'=16] {'head'}, dimensions={0} | all-to-all | bytes 5242880 | tf_op jit(solution)/shard_map/all_to_all | solution.py:106
  (53 shorter events, 40.7 us)
Async XLA Ops:
  7.8 10.8 %all-to-all-start.1 = ((bf16[256,2,4]{0,2,1:T(4,128)(2,1)}), bf16[256,2,4]{0,2,1:T(4,128)(2,1)S(1)}, u32[]{:S(2)}, u32[]{:S(2)}) async-start(bf16[256,2,4]{0,2,1:T(4,128)(2,1)} %all_to_all.61), calls=%async_computation.1 | async-start | bytes 8192 | tf_op jit(solution)/shard_map/all_to_all | solution.py:53
  18.6 34.8 %all-to-all-start = ((bf16[256,2,2560]{2,0,1:T(8,128)(2,1)}), bf16[256,2,2560]{2,0,1:T(8,128)(2,1)S(1)}, u32[]{:S(2)}, u32[]{:S(2)}) async-start(bf16[256,2,2560]{2,0,1:T(8,128)(2,1)} %bitcast.130), calls=%async_computation | async-start | bytes 5242880 | tf_op jit(solution)/shard_map/all_to_all | solution.py:51
  53.4 35.2 %all-to-all-start.2 = ((bf16[256,2,2560]{2,0,1:T(8,128)(2,1)}), bf16[256,2,2560]{2,0,1:T(8,128)(2,1)}, u32[]{:S(2)}, u32[]{:S(2)}) async-start(bf16[256,2,2560]{2,0,1:T(8,128)(2,1)} %bitcast.129), calls=%async_computation.2 | async-start | bytes 5242880 | tf_op jit(solution)/shard_map/all_to_all | solution.py:52
  58.4 425.2 %all-reduce.3.cloned.1.call-start = ((), (), s32[]{:S(2)}) async-start(), calls=%async_computation.5 | async-start | bytes 39321600 | tf_op jit(solution)/shard_map/psum | solution.py:85
  100.6 12.3 %slice-start = ((s8[5242880]{0:T(1024)(128)(4,1)}), s8[4194304]{0:T(1024)(128)(4,1)S(1)}, s32[]{:S(2)}) async-start(s8[5242880]{0:T(1024)(128)(4,1)} %bitcast.126), calls=%async_computation.6 | async-start | bytes 8388608
  100.6 13.5 %slice-start.2 = ((s8[6553600]{0:T(1024)(128)(4,1)}), s8[4194304]{0:T(1024)(128)(4,1)S(1)}, s32[]{:S(2)}) async-start(s8[6553600]{0:T(1024)(128)(4,1)} %bitcast.136), calls=%async_computation.8 | async-start | bytes 8388608
  105.6 7.4 %slice-start.1 = ((s8[5242880]{0:T(1024)(128)(4,1)}), s8[1048576]{0:T(1024)(128)(4,1)S(1)}, s32[]{:S(2)}) async-start(s8[5242880]{0:T(1024)(128)(4,1)} %bitcast.126), calls=%async_computation.7 | async-start | bytes 2097152
  105.6 8.5 %slice-start.3 = ((s8[6553600]{0:T(1024)(128)(4,1)}), s8[2359296]{0:T(1024)(128)(4,1)S(1)}, s32[]{:S(2)}) async-start(s8[6553600]{0:T(1024)(128)(4,1)} %bitcast.136), calls=%async_computation.9 | async-start | bytes 4718592
  118.6 8.1 %copy-start.3 = (f32[4,512,640]{2,1,0:T(8,128)S(1)}, f32[4,512,640]{2,1,0:T(8,128)}, u32[]{:S(2)}) copy-start(f32[4,512,640]{2,1,0:T(8,128)} %fusion.30) | copy-start | bytes 15728644
  142.1 1.7 copy-start.1
  142.1 2.3 copy-start.4
  483.6 6.6 copy-start.2
  510.1 11.2 %slice-start.4 = ((s8[6553600]{0:T(1024)(128)(4,1)}), s8[4194304]{0:T(1024)(128)(4,1)S(1)}, s32[]{:S(2)}) async-start(s8[6553600]{0:T(1024)(128)(4,1)} %bitcast.138), calls=%async_computation.10 | async-start | bytes 8388608
  516.3 5.0 slice-start.5
  547.7 1.7 copy-start
Sparse Core Ops, SparseCore 0:
  142.2 341.3 all-reduce.2
where the time goes:
time: 694 us; the launch traced here: 687 us
  waiting for transfers between devices  355 us (51%)
  matrix products  180 us (26%)
  blocking collectives  65.3 us (9%)
  local copies, waits for them, and re-layouts  34 us (5%)
  other arithmetic  24.7 us (4%)
  between operations  14 us (2%)
  starting transfers between devices  13.2 us (2%)
    psum x1, waiting for transfers between devices, per_device(): lax.psum((grad_first, grad_second, grad_third), 'ctx')  304 us
    dot_general x3, matrix products, update_rows(): jnp.einsum('hij,hjk->hik', polynomial, full_iterate, preferred_element_ty...  42.8 us
    dot_general x6, matrix products, orthogonal(): jnp.einsum('hij,hkj->hik', iterate, iterate, preferred_element_type=jnp.f...  36.1 us
    all_to_all x1, blocking collectives, per_device(): lax.all_to_all(normed.reshape(token_rows, heads_here * width), 'head', sp...  33 us
    all_to_all x1, blocking collectives, per_device(): lax.all_to_all(queries_n, 'head', split_axis=1, concat_axis=0, tiled=True)  32.2 us
    all_to_all x1, waiting for transfers between devices, per_device(): lax.all_to_all(keys_n, 'head', split_axis=1, concat_axis=0, tiled=True)  27.5 us
    all_to_all x1, waiting for transfers between devices, per_device(): lax.all_to_all(values, 'head', split_axis=1, concat_axis=0, tiled=True)  23.8 us
    dot_general x1, matrix products, per_device(): jnp.einsum('thd,hde->the', query_local, new_first, preferred_element_type...  16.2 us
  transfers between devices with their start and end apart: 4, of which 3 were waited for; matrix products, arithmetic and copies ran while one was open for 3% of the time, Pallas kernels for 0%

commit v1 on v0

v1 whole, which is shorter than its diff:
```python
import functools

import jax
import jax.numpy as jnp
from jax import lax
from jax.experimental import pallas as pl
from jax.experimental.pallas import tpu as pltpu
from jax.sharding import Mesh, PartitionSpec as P


NS_STEPS = 2

epsilon = 1e-06
frob_eps = 1e-07
coeff_a = 3.4445
coeff_b = -4.775
coeff_c = 2.0315
step_size = 1.0

f32 = jnp.float32
bf16 = jnp.bfloat16
NT = (((1,), (1,)), ((), ()))


def mm(a, b):
    return jnp.dot(a, b, preferred_element_type=f32)


def cost(flops, moved):
    return pl.CostEstimate(flops=flops, bytes_accessed=moved, transcendentals=0)


def normalized(x_ref, gain_ref, out_ref, place):
    heads, width = out_ref.shape[0], out_ref.shape[-1]
    wide = x_ref[...].astype(f32)
    factor = lax.rsqrt(jnp.mean(wide * wide, axis=-1, keepdims=True) + epsilon)
    for head in range(heads):
        cols = slice(head * width, (head + 1) * width)
        out_ref[place(head)] = (
            x_ref[:, cols].astype(f32) * factor * gain_ref[:, cols]
        ).astype(bf16)


def query_kernel(x_ref, gain_ref, out_ref):
    normalized(x_ref, gain_ref, out_ref, lambda head: head)


def pair_kernel(k_ref, v_ref, rate_ref, gain_ref, out_ref):
    heads, width = out_ref.shape[0], out_ref.shape[-1]
    normalized(k_ref, gain_ref, out_ref, lambda head: (head, 0))
    for head in range(heads):
        cols = slice(head * width, (head + 1) * width)
        rate = rate_ref[:, head : head + 1].astype(f32)
        out_ref[head, 1] = (v_ref[:, cols].astype(f32) * rate).astype(bf16)


def prepared_queries(x, gain, heads):
    rows, model = x.shape
    width = model // heads
    block = rows // 4 if rows % 64 == 0 else rows
    return pl.pallas_call(
        query_kernel,
        grid=(rows // block,),
        in_specs=[
            pl.BlockSpec((block, model), lambda i: (i, 0)),
            pl.BlockSpec((1, model), lambda i: (0, 0)),
        ],
        out_specs=pl.BlockSpec((heads, block, width), lambda i: (0, i, 0)),
        out_shape=jax.ShapeDtypeStruct((heads, rows, width), bf16),
        cost_estimate=cost(8 * rows * model, 4 * rows * model),
    )(x, gain)


def prepared_pair(keys, values, rates, gain, first, steps, block):
    heads = rates.shape[1]
    model = keys.shape[1]
    rows = block * steps
    width = model // heads
    tile = pl.BlockSpec((block, model), lambda i: (first + i, 0))
    return pl.pallas_call(
        pair_kernel,
        grid=(steps,),
        in_specs=[
            tile,
            tile,
            pl.BlockSpec((block, heads), lambda i: (first + i, 0)),
            pl.BlockSpec((1, model), lambda i: (0, 0)),
        ],
        out_specs=pl.BlockSpec((heads, 2, block, width), lambda i: (0, 0, i, 0)),
        out_shape=jax.ShapeDtypeStruct((heads, 2, rows, width), bf16),
        cost_estimate=cost(12 * rows * model, 8 * rows * model),
    )(keys, values, rates, gain)


def back_to_columns(x):
    heads, rows, width = x.shape

    def kernel(x_ref, out_ref):
        for head in range(heads):
            out_ref[:, head * width : (head + 1) * width] = x_ref[head]

    block = rows // 4 if rows % 64 == 0 else rows
    return pl.pallas_call(
        kernel,
        grid=(rows // block,),
        in_specs=[pl.BlockSpec((heads, block, width), lambda i: (0, i, 0))],
        out_specs=pl.BlockSpec((block, heads * width), lambda i: (i, 0)),
        out_shape=jax.ShapeDtypeStruct((rows, heads * width), bf16),
        cost_estimate=cost(rows * heads * width, 4 * rows * heads * width),
    )(x)


def accumulate(pair_ref, wb1, wb2, wb3, acc1, acc2, acc3):
    sources, _, rows, width = pair_ref.shape
    keys = pair_ref[:, 0].reshape(sources * rows, width)
    scaled = pair_ref[:, 1].reshape(sources * rows, width)
    pre1 = mm(keys, wb1[...])
    pre3 = mm(keys, wb3[...])
    sigmoid = jax.nn.sigmoid(pre1)
    activ = pre1 * sigmoid
    hidden = (activ * pre3).astype(bf16)
    back = mm(scaled, wb2[...])
    d1 = (back * pre3 * sigmoid * (1.0 + pre1 * (1.0 - sigmoid))).astype(bf16)
    d3 = (back * activ).astype(bf16)
    keys_t = keys.T
    acc1[...] += mm(keys_t, d1)
    acc3[...] += mm(keys_t, d3)
    acc2[...] += mm(hidden.T, scaled)


def first_kernel(
    ids, pair_ref, w1_ref, w2_ref, w3_ref, acc1, acc2, acc3, wb1, wb2, wb3
):
    @pl.when(pl.program_id(0) == 0)
    def _():
        wb1[...] = w1_ref[0].astype(bf16)
        wb2[...] = w2_ref[0].astype(bf16).T
        wb3[...] = w3_ref[0].astype(bf16)
        for acc in (acc1, acc2, acc3):
            acc[...] = jnp.zeros_like(acc)

    accumulate(pair_ref, wb1, wb2, wb3, acc1, acc2, acc3)


def last_kernel(
    ids, pair_ref, was1, was2, was3, wb1, wb2, wb3,
    send1, keep1, send2, keep2, send3, keep3, acc1, acc2, acc3,
):
    @pl.when(pl.program_id(0) == 0)
    def _():
        for acc in (acc1, acc2, acc3):
            acc[...] = jnp.zeros_like(acc)

    accumulate(pair_ref, wb1, wb2, wb3, acc1, acc2, acc3)

    @pl.when(pl.program_id(0) == pl.num_programs(0) - 1)
    def _():
        half = keep1.shape[0]
        mine = pl.ds(pl.multiple_of(ids[1] * half, 16), half)
        other = pl.ds(pl.multiple_of((1 - ids[1]) * half, 16), half)
        for was, acc, send, keep in (
            (was1, acc1, send1, keep1),
            (was2, acc2, send2, keep2),
            (was3, acc3, send3, keep3),
        ):
            send[...] = (was[other, :] + acc[other, :]).astype(bf16)
            keep[...] = was[mine, :] + acc[mine, :]


def grad_call(kernel, ids, pair, others, other_specs, outs, out_specs, scratch):
    heads, _, rows, width = pair.shape
    sources = heads // 2 if heads % 2 == 0 else heads
    return pl.pallas_call(
        kernel,
        grid_spec=pltpu.PrefetchScalarGridSpec(
            num_scalar_prefetch=1,
            grid=(heads // sources,),
            in_specs=[pl.BlockSpec((sources, 2, rows, width), lambda i, ids: (i, 0, 0, 0))]
            + other_specs,
            out_specs=out_specs,
            scratch_shapes=scratch,
        ),
        out_shape=outs,
        cost_estimate=cost(12 * heads * rows * width * width, 4 * heads * rows * width),
        compiler_params=pltpu.CompilerParams(vmem_limit_bytes=60 << 20),
    )(ids, pair, *others)


def gradients_first(ids, pair, weights):
    width = pair.shape[-1]
    weight = pl.BlockSpec((1, width, width), lambda i, ids: (ids[0], 0, 0))
    full = pl.BlockSpec((width, width), lambda i, ids: (0, 0))
    outs = [jax.ShapeDtypeStruct((width, width), f32)] * 3
    outs += [jax.ShapeDtypeStruct((width, width), bf16)] * 3
    return grad_call(first_kernel, ids, pair, weights, [weight] * 3, outs, [full] * 6, [])


def gradients_last(ids, pair, carried):
    width = pair.shape[-1]
    rows = width // 2
    full = pl.BlockSpec((width, width), lambda i, ids: (0, 0))
    half = pl.BlockSpec((rows, width), lambda i, ids: (0, 0))
    outs = [
        jax.ShapeDtypeStruct((rows, width), bf16),
        jax.ShapeDtypeStruct((rows, width), f32),
    ] * 3
    scratch = [pltpu.VMEM((width, width), f32)] * 3
    return grad_call(last_kernel, ids, pair, carried, [full] * 6, outs, [half] * 6, scratch)


def newton_kernel(ids, g_ref, w_ref, u_ref):
    grad = g_ref[...].astype(f32)
    total = jnp.sqrt(jnp.sum(grad * grad))
    x = (grad / (total + frob_eps)).astype(bf16)
    for _ in range(NS_STEPS):
        square = lax.dot_general(x, x, NT, preferred_element_type=f32).astype(bf16)
        poly = (coeff_b * square.astype(f32) + coeff_c * mm(square, square)).astype(bf16)
        x = (coeff_a * x.astype(f32) + mm(poly, x)).astype(bf16)
    u_ref[...] = (w_ref[0] + step_size * x.astype(f32)).astype(bf16)


def updated(ids, grad, weight):
    width = grad.shape[0]
    full = pl.BlockSpec((width, width), lambda i, ids: (0, 0))
    return pl.pallas_call(
        newton_kernel,
        grid_spec=pltpu.PrefetchScalarGridSpec(
            num_scalar_prefetch=1,
            grid=(1,),
            in_specs=[full, pl.BlockSpec((1, width, width), lambda i, ids: (ids[0], 0, 0))],
            out_specs=full,
        ),
        out_shape=jax.ShapeDtypeStruct((width, width), bf16),
        cost_estimate=cost(12 * width**3, 8 * width * width),
        compiler_params=pltpu.CompilerParams(vmem_limit_bytes=60 << 20),
    )(ids, grad, weight)


def gate_kernel(q_ref, u1_ref, u3_ref, f_ref):
    pre1 = mm(q_ref[...], u1_ref[...])
    pre3 = mm(q_ref[...], u3_ref[...])
    f_ref[...] = (pre1 * jax.nn.sigmoid(pre1) * pre3).astype(bf16)


def output_kernel(f_ref, u2_ref, o_ref):
    out = mm(f_ref[...], u2_ref[...])
    factor = lax.rsqrt(jnp.mean(out * out, axis=-1, keepdims=True) + epsilon)
    o_ref[...] = (out * factor).astype(bf16)


def over_tokens(kernel, x, *weights):
    tokens, width = x.shape
    block = tokens // 4
    tile = pl.BlockSpec((block, width), lambda i: (i, 0))
    full = pl.BlockSpec((width, width), lambda i: (0, 0))
    return pl.pallas_call(
        kernel,
        grid=(tokens // block,),
        in_specs=[tile] + [full] * len(weights),
        out_specs=tile,
        out_shape=jax.ShapeDtypeStruct((tokens, width), bf16),
        cost_estimate=cost(2 * len(weights) * tokens * width * width, 4 * tokens * width),
        compiler_params=pltpu.CompilerParams(vmem_limit_bytes=60 << 20),
    )(x, *weights)


def summed(send, keep, steps):
    for place, (axis, size, bit) in enumerate(steps):
        pairs = [(i, i ^ (1 << bit)) for i in range(size)]
        came = lax.ppermute(send, axis, pairs)
        keep = keep + came.astype(f32)
        if place + 1 == len(steps):
            whole = keep.astype(bf16)
            break
        axis, size, bit = steps[place + 1]
        rows = keep.shape[0] // 2
        side = (lax.axis_index(axis) >> bit) & 1
        send = lax.dynamic_slice_in_dim(keep, (1 - side) * rows, rows, 0).astype(bf16)
        keep = lax.dynamic_slice_in_dim(keep, side * rows, rows, 0)
    for place, (axis, size, bit) in reversed(list(enumerate(steps))):
        pairs = [(i, i ^ (1 << bit)) for i in range(size)]
        other = lax.ppermute(whole, axis, pairs)
        first = ((lax.axis_index(axis) >> bit) & 1) == 0
        whole = jnp.concatenate(
            [jnp.where(first, whole, other), jnp.where(first, other, whole)], axis=0
        )
    return whole


def per_device(
    sizes, queries, keys, values, rates, q_gain, k_gain, w_first, w_second, w_third
):
    heads = rates.shape[1]
    width = w_first.shape[1]
    exchange = functools.partial(
        lax.all_to_all, axis_name=("head", "l1", "l2"), split_axis=0, concat_axis=0, tiled=True
    )
    steps = [
        (axis, sizes[axis], bit)
        for axis in ("h2", "h1")
        for bit in range(sizes[axis].bit_length() - 1)
    ]
    axis, _, bit = steps[0]
    ids = jnp.stack([
        lax.axis_index("l1") * sizes["l2"] + lax.axis_index("l2"),
        (lax.axis_index(axis) >> bit) & 1,
    ]).astype(jnp.int32)
    pairs = []
    block = keys.shape[0] // 4
    for start, count in ((0, 3), (3, 1)):
        pair = prepared_pair(keys, values, rates, k_gain[None], start, count, block)
        pairs.append(exchange(pair))
    ready = prepared_queries(queries, q_gain[None], heads)
    query_local = exchange(ready)
    carried = gradients_first(ids, pairs[0], (w_first, w_second, w_third))
    s1, p1, s2, p2, s3, p3 = gradients_last(ids, pairs[1], carried)
    full_first = summed(s1, p1, steps)
    full_third = summed(s3, p3, steps)
    full_second = summed(s2, p2, steps)
    new_first = updated(ids, full_first, w_first)
    new_third = updated(ids, full_third, w_third)
    gated = over_tokens(gate_kernel, query_local.reshape(-1, width), new_first, new_third)
    new_second = updated(ids, full_second, w_second)
    normed = over_tokens(output_kernel, gated, new_second)
    return back_to_columns(exchange(normed.reshape(heads, -1, width)))


def solution(mesh):
    head, ctx = mesh.shape["head"], mesh.shape["ctx"]

    def run(queries, keys, values, rates, q_gain, k_gain, w_first, w_second, w_third):
        lo = w_first.shape[0] // head
        hi = ctx // lo
        sizes = {"l2": min(lo, 2), "h2": min(hi, 2)}
        sizes["l1"] = lo // sizes["l2"]
        sizes["h1"] = hi // sizes["h2"]
        assert hi > 1 and hi * lo == ctx and ctx & (ctx - 1) == 0
        assert w_first.shape[1] % (2 * hi) == 0
        order = ("h1", "l1", "h2", "l2")
        shape = [head] + [sizes[axis] for axis in order]
        inner = Mesh(mesh.devices.reshape(shape), ("head",) + order)
        tokens = P(("head",) + order, None)
        return jax.shard_map(
            functools.partial(per_device, sizes),
            mesh=inner,
            in_specs=(tokens,) * 4 + (P(), P()) + (P("head", None, None),) * 3,
            out_specs=tokens,
            check_vma=False,
        )(queries, keys, values, rates, q_gain, k_gain, w_first, w_second, w_third)

    return run
```

time: 694 us -> 280 us (0.40)
  waiting for transfers between devices: 355 us -> 106 us
  matrix products: 180 us -> 0 us
  Pallas kernels: 0 us -> 84.6 us
  local copies, waits for them, and re-layouts: 34 us -> 4.1 us
  blocking collectives: 65.3 us -> 36.6 us
  starting transfers between devices: 13.2 us -> 41.4 us
  other arithmetic: 24.7 us -> 6.84 us
  between operations: 14 us -> 0.16 us
    psum x1 -> x0, waiting for transfers between devices: 304 us -> none  [per_device(): lax.psum((grad_first, grad_second, grad_third), 'ctx')]
    dot_general x21 -> x0, matrix products: 180 us -> none  [the longest x3 42.8 us: update_rows(): jnp.einsum('hij,hjk->hik', polynomial, full_iterate, preferred_element_ty...]
    pallas_call x0 -> x11, Pallas kernels: none -> 84.6 us  [the longest x2 28 us: grad_call(): pl.pallas_call(kernel, grid_spec=pltpu.PrefetchScalarGridSpec(num_scalar_...]
    ppermute x0 -> x12, waiting for transfers between devices: none -> 61.8 us  [the longest x6 40.1 us: summed(): other = lax.ppermute(whole, axis, pairs)]
    all_to_all x2 -> x1, blocking collectives: 65.3 us -> 36.6 us  [per_device(): return back_to_columns(exchange(normed.reshape(heads, -1, width)))]
    ppermute x0 -> x12, starting transfers between devices: none -> 28.7 us  [the longest x6 15.2 us: summed(): other = lax.ppermute(whole, axis, pairs)]
    all_to_all x7 -> x0, local copies, waits for them, and re-layouts: 14.2 us -> none  [the longest x3 7.61 us: per_device(): lax.all_to_all(normed.reshape(token_rows, heads_here * width), 'head', sp...]
    reduce_sum x4 -> x0, other arithmetic: 12.3 us -> none  [the longest x2 9.37 us: orthogonal(): jnp.sum(gradient * gradient, axis=(1, 2), keepdims=True)]
  transfers between devices with their start and end apart: 4 -> 15, of which waited for: 3 -> 14; matrix products, arithmetic and copies ran while one was open for 3% -> 2% of each run, Pallas kernels for 0% -> 18%
where the time goes in v1:
time: 280 us; the launch traced here: 279 us
  waiting for transfers between devices  106 us (38%)
  Pallas kernels  84.6 us (30%)
  starting transfers between devices  41.4 us (15%)
  blocking collectives  36.6 us (13%)
  other arithmetic  6.84 us (2%)
  local copies, waits for them, and re-layouts  4.1 us (1%)
    all_to_all x2, waiting for transfers between devices, per_device(): pairs.append(exchange(pair))  43.8 us
    ppermute x6, waiting for transfers between devices, summed(): other = lax.ppermute(whole, axis, pairs)  40.1 us
    all_to_all x1, blocking collectives, per_device(): return back_to_columns(exchange(normed.reshape(heads, -1, width)))  36.6 us
    pallas_call x2, Pallas kernels, grad_call(): pl.pallas_call(kernel, grid_spec=pltpu.PrefetchScalarGridSpec(num_scalar_...  28 us
    pallas_call x3, Pallas kernels, updated(): pl.pallas_call(newton_kernel, grid_spec=pltpu.PrefetchScalarGridSpec(num_...  25.4 us
    ppermute x6, waiting for transfers between devices, summed(): came = lax.ppermute(send, axis, pairs)  21.7 us
    ppermute x6, starting transfers between devices, summed(): other = lax.ppermute(whole, axis, pairs)  15.2 us
    pallas_call x2, Pallas kernels, over_tokens(): pl.pallas_call(kernel, grid=(tokens // block,), in_specs=[tile] + [full]...  14 us
  transfers between devices with their start and end apart: 15, of which 14 were waited for; matrix products, arithmetic and copies ran while one was open for 2% of the time, Pallas kernels for 18%

profile of v1, /device:TPU:0, one launch (start us, length us, event | category | flops | bytes accessed | tf_op | source)
XLA Modules:
  0.0 279.2 jit_solution(18356042493105611649)
XLA Ops:
  1.4 5.8 %shard_map.93 = bf16[8,2,192,640]{3,2,1,0:T(8,128)(2,1)} custom-call(bf16[256,5120]{1,0:T(8,128)(2,1)} %k_ref.3, bf16[256,5120]{1,0:T(8,128)(2,1)} %v_ref.3, bf16[256,8]{1,0:T(8,128)(2,1)} %copy.10.rate_ref, f32[1,5120]{1,0:T(1,128)} %bitcast.8), custom_call_target="tpu_custom_call" | custom-call | flops 11796480 | bytes 7864320 | tf_op jit(solution)/shard_map/pallas_call | solution.py:80
  7.2 5.3 %all-to-all-start.2 = ((bf16[8,2,192,640]{3,2,1,0:T(8,128)(2,1)}), bf16[8,2,192,640]{3,2,1,0:T(8,128)(2,1)}, u32[]{:S(2)}, u32[]{:S(2)}) async-start(bf16[8,2,192,640]{3,2,1,0:T(8,128)(2,1)} %shard_map.93), calls=%async_computation.2 | async-start | bytes 7864320 | tf_op jit(solution)/shard_map/all_to_all | solution.py:312
  12.4 2.9 %shard_map.92 = bf16[8,2,64,640]{3,2,1,0:T(8,128)(2,1)} custom-call(bf16[256,5120]{1,0:T(8,128)(2,1)} %k_ref.3, bf16[256,5120]{1,0:T(8,128)(2,1)} %v_ref.3, bf16[256,8]{1,0:T(8,128)(2,1)} %copy.10.rate_ref, f32[1,5120]{1,0:T(1,128)} %bitcast.9), custom_call_target="tpu_custom_call" | custom-call | flops 3932160 | bytes 2621440 | tf_op jit(solution)/shard_map/pallas_call | solution.py:80
  15.3 43.5 %all-to-all-done.2.pair_ref = bf16[8,2,192,640]{3,2,1,0:T(8,128)(2,1)} async-done(((bf16[8,2,192,640]{3,2,1,0:T(8,128)(2,1)}), bf16[8,2,192,640]{3,2,1,0:T(8,128)(2,1)}, u32[]{:S(2)}, u32[]{:S(2)}) %all-to-all-start.2) | async-done | bytes 3932192 | tf_op jit(solution)/shard_map/all_to_all | solution.py:312
  58.8 3.6 %all-to-all-start.1 = ((bf16[8,2,64,640]{3,2,1,0:T(8,128)(2,1)}), bf16[8,2,64,640]{3,2,1,0:T(8,128)(2,1)S(1)}, u32[]{:S(2)}, u32[]{:S(2)}) async-start(bf16[8,2,64,640]{3,2,1,0:T(8,128)(2,1)} %shard_map.92), calls=%async_computation.1 | async-start | bytes 2621440 | tf_op jit(solution)/shard_map/all_to_all | solution.py:312
  63.0 17.2 %shard_map.94 = (f32[640,640]{1,0:T(8,128)}, f32[640,640]{1,0:T(8,128)}, f32[640,640]{1,0:T(8,128)}, bf16[640,640]{1,0:T(8,128)(2,1)}, bf16[640,640]{1,0:T(8,128)(2,1)}, /*index=5*/bf16[640,640]{1,0:T(8,128)(2,1)}) custom-call(s32[2]{0:T(128)} %pad_add_fusion.ids, bf16[8,2,192,640]{3,2,1,0:T(8,128)(2,1)} %all-to-all-done.2.pair_ref, f32[4,640,640]{2,1,0:T(8,128)} %w_ref.3, ...), custom_call_target="tpu_custom_call" | custom-call | flops 7549747200 | bytes 3932160 | tf_op jit(solution)/shard_map/pallas_call | solution.py:173
  81.6 10.8 %shard_map.95 = (bf16[320,640]{1,0:T(8,128)(2,1)}, f32[320,640]{1,0:T(8,128)}, bf16[320,640]{1,0:T(8,128)(2,1)}, f32[320,640]{1,0:T(8,128)}, bf16[320,640]{1,0:T(8,128)(2,1)}, /*index=5*/f32[320,640]{1,0:T(8,128)}) custom-call(s32[2]{0:T(128)} %pad_add_fusion.ids, bf16[8,2,64,640]{3,2,1,0:T(8,128)(2,1)} %copy-done.1, f32[640,640]{1,0:T(8,128)} %get-tuple-element.17.was1, ...), custom_call_target="tpu_custom_call" | custom-call | flops 2516582400 | bytes 1310720 | tf_op jit(solution)/shard_map/pallas_call | solution.py:173
  92.4 2.2 collective-permute-start.8
  94.6 4.5 %shard_map.91 = bf16[8,256,640]{2,1,0:T(8,128)(2,1)} custom-call(bf16[256,5120]{1,0:T(8,128)(2,1)} %x_ref.1, f32[1,5120]{1,0:T(1,128)} %bitcast.10), custom_call_target="tpu_custom_call" | custom-call | flops 10485760 | bytes 5242880 | tf_op jit(solution)/shard_map/pallas_call | solution.py:61
  99.2 3.8 %all-to-all-start = ((bf16[8,256,640]{2,1,0:T(8,128)(2,1)}), bf16[8,256,640]{2,1,0:T(8,128)(2,1)S(1)}, u32[]{:S(2)}, u32[]{:S(2)}) async-start(bf16[8,256,640]{2,1,0:T(8,128)(2,1)} %shard_map.91), calls=%async_computation | async-start | bytes 5242880 | tf_op jit(solution)/shard_map/all_to_all | solution.py:314
  106.6 3.2 %collective-permute-start.9 = (bf16[160,640]{1,0:T(8,128)(2,1)S(1)}, bf16[160,640]{1,0:T(8,128)(2,1)S(1)}, u32[]{:S(2)}, u32[]{:S(2)}) collective-permute-start(bf16[160,640]{1,0:T(8,128)(2,1)S(1)} %dynamic-slice_convert_fusion), channel_id=1, source_target_pairs={{0,8},{8,0},{1,9},{9,1},{2,10},{10,2},{3,11},{11,3},{4,12},{12,4},... | collective-permute-start | bytes 614408 | tf_op jit(solution)/shard_map/ppermute | solution.py:270
  109.7 4.3 %collective-permute-done.4 = bf16[320,640]{1,0:T(8,128)(2,1)} collective-permute-done((bf16[320,640]{1,0:T(8,128)(2,1)}, bf16[320,640]{1,0:T(8,128)(2,1)}, u32[]{:S(2)}, u32[]{:S(2)}) %collective-permute-start.4) | collective-permute-done | bytes 409632 | tf_op jit(solution)/shard_map/ppermute | solution.py:270
  115.1 3.2 %collective-permute-start.5 = (bf16[160,640]{1,0:T(8,128)(2,1)S(1)}, bf16[160,640]{1,0:T(8,128)(2,1)S(1)}, u32[]{:S(2)}, u32[]{:S(2)}) collective-permute-start(bf16[160,640]{1,0:T(8,128)(2,1)S(1)} %dynamic-slice_convert_fusion.1), channel_id=1, source_target_pairs={{0,8},{8,0},{1,9},{9,1},{2,10},{10,2},{3,11},{11,3},{4,12},{12,4},... | collective-permute-start | bytes 614408 | tf_op jit(solution)/shard_map/ppermute | solution.py:270
  118.3 3.8 %collective-permute-done = bf16[320,640]{1,0:T(8,128)(2,1)S(1)} collective-permute-done((bf16[320,640]{1,0:T(8,128)(2,1)}, bf16[320,640]{1,0:T(8,128)(2,1)S(1)}, u32[]{:S(2)}, u32[]{:S(2)}) %collective-permute-start) | collective-permute-done | bytes 409632 | tf_op jit(solution)/shard_map/ppermute | solution.py:270
  122.2 2.9 %collective-permute-start.1 = (bf16[160,640]{1,0:T(8,128)(2,1)S(1)}, bf16[160,640]{1,0:T(8,128)(2,1)S(1)}, u32[]{:S(2)}, u32[]{:S(2)}) collective-permute-start(bf16[160,640]{1,0:T(8,128)(2,1)S(1)} %dynamic-slice_convert_fusion.2), channel_id=1, source_target_pairs={{0,8},{8,0},{1,9},{9,1},{2,10},{10,2},{3,11},{11,3},{4,12},{12,4},... | collective-permute-start | bytes 614408 | tf_op jit(solution)/shard_map/ppermute | solution.py:270
  125.1 11.8 %collective-permute-done.9 = bf16[160,640]{1,0:T(8,128)(2,1)S(1)} collective-permute-done((bf16[160,640]{1,0:T(8,128)(2,1)S(1)}, bf16[160,640]{1,0:T(8,128)(2,1)S(1)}, u32[]{:S(2)}, u32[]{:S(2)}) %collective-permute-start.9) | collective-permute-done | bytes 204832 | tf_op jit(solution)/shard_map/ppermute | solution.py:270
  136.9 3.4 %collective-permute-start.10 = (bf16[160,640]{1,0:T(8,128)(2,1)S(1)}, bf16[160,640]{1,0:T(8,128)(2,1)S(1)}, u32[]{:S(2)}, u32[]{:S(2)}) collective-permute-start(bf16[160,640]{1,0:T(8,128)(2,1)S(1)} %add_convert_fusion), channel_id=1, source_target_pairs={{0,8},{8,0},{1,9},{9,1},{2,10},{10,2},{3,11},{11,3},{4,12},{12,4},... | collective-permute-start | bytes 614408 | tf_op jit(solution)/shard_map/ppermute | solution.py:282
  141.3 3.5 %collective-permute-start.6 = (bf16[160,640]{1,0:T(8,128)(2,1)S(1)}, bf16[160,640]{1,0:T(8,128)(2,1)S(1)}, u32[]{:S(2)}, u32[]{:S(2)}) collective-permute-start(bf16[160,640]{1,0:T(8,128)(2,1)S(1)} %add_convert_fusion.1), channel_id=1, source_target_pairs={{0,8},{8,0},{1,9},{9,1},{2,10},{10,2},{3,11},{11,3},{4,12},{12,4},... | collective-permute-start | bytes 614408 | tf_op jit(solution)/shard_map/ppermute | solution.py:282
  145.7 3.5 %collective-permute-start.2 = (bf16[160,640]{1,0:T(8,128)(2,1)S(1)}, bf16[160,640]{1,0:T(8,128)(2,1)S(1)}, u32[]{:S(2)}, u32[]{:S(2)}) collective-permute-start(bf16[160,640]{1,0:T(8,128)(2,1)S(1)} %add_convert_fusion.2), channel_id=1, source_target_pairs={{0,8},{8,0},{1,9},{9,1},{2,10},{10,2},{3,11},{11,3},{4,12},{12,4},... | collective-permute-start | bytes 614408 | tf_op jit(solution)/shard_map/ppermute | solution.py:282
  149.2 18.4 %collective-permute-done.10 = bf16[160,640]{1,0:T(8,128)(2,1)S(1)} collective-permute-done((bf16[160,640]{1,0:T(8,128)(2,1)S(1)}, bf16[160,640]{1,0:T(8,128)(2,1)S(1)}, u32[]{:S(2)}, u32[]{:S(2)}) %collective-permute-start.10) | collective-permute-done | bytes 204832 | tf_op jit(solution)/shard_map/ppermute | solution.py:282
  169.3 2.7 collective-permute-done.6
  173.7 2.6 collective-permute-done.2
  178.0 2.1 collective-permute-done.11
  181.2 7.6 %collective-permute-done.7 = bf16[320,640]{1,0:T(8,128)(2,1)S(1)} collective-permute-done((bf16[320,640]{1,0:T(8,128)(2,1)S(1)}, bf16[320,640]{1,0:T(8,128)(2,1)S(1)}, u32[]{:S(2)}, u32[]{:S(2)}) %collective-permute-start.7) | collective-permute-done | bytes 409632 | tf_op jit(solution)/shard_map/ppermute | solution.py:282
  190.1 6.6 %collective-permute-done.3 = bf16[320,640]{1,0:T(8,128)(2,1)S(1)} collective-permute-done((bf16[320,640]{1,0:T(8,128)(2,1)S(1)}, bf16[320,640]{1,0:T(8,128)(2,1)S(1)}, u32[]{:S(2)}, u32[]{:S(2)}) %collective-permute-start.3) | collective-permute-done | bytes 409632 | tf_op jit(solution)/shard_map/ppermute | solution.py:282
  197.8 8.4 %shard_map.99.u2_ref = bf16[640,640]{1,0:T(8,128)(2,1)} custom-call(s32[2]{0:T(128)} %pad_add_fusion.ids, bf16[640,640]{1,0:T(8,128)(2,1)} %pad_maximum_fusion.2.g_ref, f32[4,640,640]{2,1,0:T(8,128)} %w_ref.5), custom_call_target="tpu_custom_call" | custom-call | flops 3145728000 | bytes 3276800 | tf_op jit(solution)/shard_map/pallas_call | solution.py:225
  206.2 8.4 %shard_map.97.u3_ref = bf16[640,640]{1,0:T(8,128)(2,1)} custom-call(s32[2]{0:T(128)} %pad_add_fusion.ids, bf16[640,640]{1,0:T(8,128)(2,1)} %pad_maximum_fusion.1.g_ref, f32[4,640,640]{2,1,0:T(8,128)} %w_ref.4), custom_call_target="tpu_custom_call" | custom-call | flops 3145728000 | bytes 3276800 | tf_op jit(solution)/shard_map/pallas_call | solution.py:225
  214.6 8.7 %shard_map.96.u1_ref = bf16[640,640]{1,0:T(8,128)(2,1)} custom-call(s32[2]{0:T(128)} %pad_add_fusion.ids, bf16[640,640]{1,0:T(8,128)(2,1)} %pad_maximum_fusion.g_ref, f32[4,640,640]{2,1,0:T(8,128)} %w_ref.3), custom_call_target="tpu_custom_call" | custom-call | flops 3145728000 | bytes 3276800 | tf_op jit(solution)/shard_map/pallas_call | solution.py:225
  224.7 7.8 %shard_map.98.f_ref = bf16[2048,640]{1,0:T(8,128)(2,1)} custom-call(bf16[2048,640]{1,0:T(8,128)(2,1)} %bitcast.6, bf16[640,640]{1,0:T(8,128)(2,1)} %shard_map.96.u1_ref, bf16[640,640]{1,0:T(8,128)(2,1)} %shard_map.97.u3_ref), custom_call_target="tpu_custom_call" | custom-call | flops 3355443200 | bytes 5242880 | tf_op jit(solution)/shard_map/pallas_call | solution.py:256
  232.5 6.2 %shard_map.100 = bf16[2048,640]{1,0:T(8,128)(2,1)} custom-call(bf16[2048,640]{1,0:T(8,128)(2,1)} %shard_map.98.f_ref, bf16[640,640]{1,0:T(8,128)(2,1)} %shard_map.99.u2_ref), custom_call_target="tpu_custom_call" | custom-call | flops 1677721600 | bytes 5242880 | tf_op jit(solution)/shard_map/pallas_call | solution.py:256
  238.7 36.6 %all_to_all.20.x_ref = bf16[8,256,640]{2,1,0:T(8,128)(2,1)} all-to-all(bf16[8,256,640]{2,1,0:T(8,128)(2,1)} %bitcast.7), channel_id=1, replica_groups=mesh['head'=2,'h1'=2,'l1'=2,'h2'=2,'l2'=2] {'head','l1','l2'}, dimensions={0} | all-to-all | bytes 5242880 | tf_op jit(solution)/shard_map/all_to_all | solution.py:325
  275.2 4.0 %shard_map.101 = bf16[256,5120]{1,0:T(8,128)(2,1)} custom-call(bf16[8,256,640]{2,1,0:T(8,128)(2,1)} %all_to_all.20.x_ref), custom_call_target="tpu_custom_call" | custom-call | flops 1310720 | bytes 5242880 | tf_op jit(solution)/shard_map/pallas_call | solution.py:103
  (41 shorter events, 20.0 us)
Async XLA Ops:
  7.2 51.6 %all-to-all-start.2 = ((bf16[8,2,192,640]{3,2,1,0:T(8,128)(2,1)}), bf16[8,2,192,640]{3,2,1,0:T(8,128)(2,1)}, u32[]{:S(2)}, u32[]{:S(2)}) async-start(bf16[8,2,192,640]{3,2,1,0:T(8,128)(2,1)} %shard_map.93), calls=%async_computation.2 | async-start | bytes 7864320 | tf_op jit(solution)/shard_map/all_to_all | solution.py:312
  58.8 21.7 %all-to-all-start.1 = ((bf16[8,2,64,640]{3,2,1,0:T(8,128)(2,1)}), bf16[8,2,64,640]{3,2,1,0:T(8,128)(2,1)S(1)}, u32[]{:S(2)}, u32[]{:S(2)}) async-start(bf16[8,2,64,640]{3,2,1,0:T(8,128)(2,1)} %shard_map.92), calls=%async_computation.1 | async-start | bytes 2621440 | tf_op jit(solution)/shard_map/all_to_all | solution.py:312
  80.5 1.1 copy-start.1
  92.4 12.8 %collective-permute-start.8 = (bf16[320,640]{1,0:T(8,128)(2,1)}, bf16[320,640]{1,0:T(8,128)(2,1)}, u32[]{:S(2)}, u32[]{:S(2)}) collective-permute-start(bf16[320,640]{1,0:T(8,128)(2,1)} %get-tuple-element.28), channel_id=1, source_target_pairs={{0,2},{2,0},{1,3},{3,1},{4,6},{6,4},{5,7},{7,5},{8,10},{10,8},{9,1... | collective-permute-start | bytes 1228808 | tf_op jit(solution)/shard_map/ppermute | solution.py:270
  94.6 19.4 %collective-permute-start.4 = (bf16[320,640]{1,0:T(8,128)(2,1)}, bf16[320,640]{1,0:T(8,128)(2,1)}, u32[]{:S(2)}, u32[]{:S(2)}) collective-permute-start(bf16[320,640]{1,0:T(8,128)(2,1)} %get-tuple-element.26), channel_id=1, source_target_pairs={{0,2},{2,0},{1,3},{3,1},{4,6},{6,4},{5,7},{7,5},{8,10},{10,8},{9,1... | collective-permute-start | bytes 1228808 | tf_op jit(solution)/shard_map/ppermute | solution.py:270
  99.2 124.0 %all-to-all-start = ((bf16[8,256,640]{2,1,0:T(8,128)(2,1)}), bf16[8,256,640]{2,1,0:T(8,128)(2,1)S(1)}, u32[]{:S(2)}, u32[]{:S(2)}) async-start(bf16[8,256,640]{2,1,0:T(8,128)(2,1)} %shard_map.91), calls=%async_computation | async-start | bytes 5242880 | tf_op jit(solution)/shard_map/all_to_all | solution.py:314
  103.0 19.1 %copy-start.2 = (f32[320,640]{1,0:T(8,128)S(1)}, f32[320,640]{1,0:T(8,128)}, u32[]{:S(2)}) copy-start(f32[320,640]{1,0:T(8,128)} %get-tuple-element.23) | copy-start | bytes 2457604
  103.0 11.0 %copy-start.3 = (f32[320,640]{1,0:T(8,128)S(1)}, f32[320,640]{1,0:T(8,128)}, u32[]{:S(2)}) copy-start(f32[320,640]{1,0:T(8,128)} %get-tuple-element.25) | copy-start | bytes 2457604
  103.0 19.0 %collective-permute-start = (bf16[320,640]{1,0:T(8,128)(2,1)}, bf16[320,640]{1,0:T(8,128)(2,1)S(1)}, u32[]{:S(2)}, u32[]{:S(2)}) collective-permute-start(bf16[320,640]{1,0:T(8,128)(2,1)} %get-tuple-element.24), channel_id=1, source_target_pairs={{0,2},{2,0},{1,3},{3,1},{4,6},{6,4},{5,7},{7,5},{8,10},{10,8},{9,1... | collective-permute-start | bytes 1228808 | tf_op jit(solution)/shard_map/ppermute | solution.py:270
  106.6 30.3 %collective-permute-start.9 = (bf16[160,640]{1,0:T(8,128)(2,1)S(1)}, bf16[160,640]{1,0:T(8,128)(2,1)S(1)}, u32[]{:S(2)}, u32[]{:S(2)}) collective-permute-start(bf16[160,640]{1,0:T(8,128)(2,1)S(1)} %dynamic-slice_convert_fusion), channel_id=1, source_target_pairs={{0,8},{8,0},{1,9},{9,1},{2,10},{10,2},{3,11},{11,3},{4,12},{12,4},... | collective-permute-start | bytes 614408 | tf_op jit(solution)/shard_map/ppermute | solution.py:270
  115.1 26.1 %collective-permute-start.5 = (bf16[160,640]{1,0:T(8,128)(2,1)S(1)}, bf16[160,640]{1,0:T(8,128)(2,1)S(1)}, u32[]{:S(2)}, u32[]{:S(2)}) collective-permute-start(bf16[160,640]{1,0:T(8,128)(2,1)S(1)} %dynamic-slice_convert_fusion.1), channel_id=1, source_target_pairs={{0,8},{8,0},{1,9},{9,1},{2,10},{10,2},{3,11},{11,3},{4,12},{12,4},... | collective-permute-start | bytes 614408 | tf_op jit(solution)/shard_map/ppermute | solution.py:270
  122.2 23.5 %collective-permute-start.1 = (bf16[160,640]{1,0:T(8,128)(2,1)S(1)}, bf16[160,640]{1,0:T(8,128)(2,1)S(1)}, u32[]{:S(2)}, u32[]{:S(2)}) collective-permute-start(bf16[160,640]{1,0:T(8,128)(2,1)S(1)} %dynamic-slice_convert_fusion.2), channel_id=1, source_target_pairs={{0,8},{8,0},{1,9},{9,1},{2,10},{10,2},{3,11},{11,3},{4,12},{12,4},... | collective-permute-start | bytes 614408 | tf_op jit(solution)/shard_map/ppermute | solution.py:270
  136.9 30.7 %collective-permute-start.10 = (bf16[160,640]{1,0:T(8,128)(2,1)S(1)}, bf16[160,640]{1,0:T(8,128)(2,1)S(1)}, u32[]{:S(2)}, u32[]{:S(2)}) collective-permute-start(bf16[160,640]{1,0:T(8,128)(2,1)S(1)} %add_convert_fusion), channel_id=1, source_target_pairs={{0,8},{8,0},{1,9},{9,1},{2,10},{10,2},{3,11},{11,3},{4,12},{12,4},... | collective-permute-start | bytes 614408 | tf_op jit(solution)/shard_map/ppermute | solution.py:282
  141.3 30.7 %collective-permute-start.6 = (bf16[160,640]{1,0:T(8,128)(2,1)S(1)}, bf16[160,640]{1,0:T(8,128)(2,1)S(1)}, u32[]{:S(2)}, u32[]{:S(2)}) collective-permute-start(bf16[160,640]{1,0:T(8,128)(2,1)S(1)} %add_convert_fusion.1), channel_id=1, source_target_pairs={{0,8},{8,0},{1,9},{9,1},{2,10},{10,2},{3,11},{11,3},{4,12},{12,4},... | collective-permute-start | bytes 614408 | tf_op jit(solution)/shard_map/ppermute | solution.py:282
  145.7 30.6 %collective-permute-start.2 = (bf16[160,640]{1,0:T(8,128)(2,1)S(1)}, bf16[160,640]{1,0:T(8,128)(2,1)S(1)}, u32[]{:S(2)}, u32[]{:S(2)}) collective-permute-start(bf16[160,640]{1,0:T(8,128)(2,1)S(1)} %add_convert_fusion.2), channel_id=1, source_target_pairs={{0,8},{8,0},{1,9},{9,1},{2,10},{10,2},{3,11},{11,3},{4,12},{12,4},... | collective-permute-start | bytes 614408 | tf_op jit(solution)/shard_map/ppermute | solution.py:282
  167.7 12.4 %collective-permute-start.11 = (bf16[320,640]{1,0:T(8,128)(2,1)S(1)}, bf16[320,640]{1,0:T(8,128)(2,1)S(1)}, u32[]{:S(2)}, u32[]{:S(2)}) collective-permute-start(bf16[320,640]{1,0:T(8,128)(2,1)S(1)} %pad_maximum_fusion.5), channel_id=1, source_target_pairs={{0,2},{2,0},{1,3},{3,1},{4,6},{6,4},{5,7},{7,5},{8,10},{10,8},{9,1... | collective-permute-start | bytes 1228808 | tf_op jit(solution)/shard_map/ppermute | solution.py:282
  172.1 16.8 %collective-permute-start.7 = (bf16[320,640]{1,0:T(8,128)(2,1)S(1)}, bf16[320,640]{1,0:T(8,128)(2,1)S(1)}, u32[]{:S(2)}, u32[]{:S(2)}) collective-permute-start(bf16[320,640]{1,0:T(8,128)(2,1)S(1)} %pad_maximum_fusion.4), channel_id=1, source_target_pairs={{0,2},{2,0},{1,3},{3,1},{4,6},{6,4},{5,7},{7,5},{8,10},{10,8},{9,1... | collective-permute-start | bytes 1228808 | tf_op jit(solution)/shard_map/ppermute | solution.py:282
  176.4 20.2 %collective-permute-start.3 = (bf16[320,640]{1,0:T(8,128)(2,1)S(1)}, bf16[320,640]{1,0:T(8,128)(2,1)S(1)}, u32[]{:S(2)}, u32[]{:S(2)}) collective-permute-start(bf16[320,640]{1,0:T(8,128)(2,1)S(1)} %pad_maximum_fusion.3), channel_id=1, source_target_pairs={{0,2},{2,0},{1,3},{3,1},{4,6},{6,4},{5,7},{7,5},{8,10},{10,8},{9,1... | collective-permute-start | bytes 1228808 | tf_op jit(solution)/shard_map/ppermute | solution.py:282
  223.2 1.5 copy-start

commit v2 on v1

--- a/solution.py
+++ b/solution.py
@@ -144,10 +144,17 @@
 
 def last_kernel(
     ids, pair_ref, was1, was2, was3, wb1, wb2, wb3,
-    send1, keep1, send2, keep2, send3, keep3, acc1, acc2, acc3,
+    send1, keep1, send2, keep2, send3, keep3, acc1, acc2, acc3, old1, old2, old3, sems,
 ):
+    loads = [
+        pltpu.make_async_copy(was, old, sems.at[i])
+        for i, (was, old) in enumerate(((was1, old1), (was2, old2), (was3, old3)))
+    ]
+
     @pl.when(pl.program_id(0) == 0)
     def _():
+        for load in loads:
+            load.start()
         for acc in (acc1, acc2, acc3):
             acc[...] = jnp.zeros_like(acc)
 
@@ -158,11 +165,12 @@
         half = keep1.shape[0]
         mine = pl.ds(pl.multiple_of(ids[1] * half, 16), half)
         other = pl.ds(pl.multiple_of((1 - ids[1]) * half, 16), half)
-        for was, acc, send, keep in (
-            (was1, acc1, send1, keep1),
-            (was2, acc2, send2, keep2),
-            (was3, acc3, send3, keep3),
+        for load, was, acc, send, keep in (
+            (loads[0], old1, acc1, send1, keep1),
+            (loads[2], old3, acc3, send3, keep3),
+            (loads[1], old2, acc2, send2, keep2),
         ):
+            load.wait()
             send[...] = (was[other, :] + acc[other, :]).astype(bf16)
             keep[...] = was[mine, :] + acc[mine, :]
 
@@ -204,11 +212,15 @@
         jax.ShapeDtypeStruct((rows, width), bf16),
         jax.ShapeDtypeStruct((rows, width), f32),
     ] * 3
-    scratch = [pltpu.VMEM((width, width), f32)] * 3
-    return grad_call(last_kernel, ids, pair, carried, [full] * 6, outs, [half] * 6, scratch)
-
-
-def newton_kernel(ids, g_ref, w_ref, u_ref):
+    scratch = [pltpu.VMEM((width, width), f32)] * 6 + [pltpu.SemaphoreType.DMA((3,))]
+    specs = [pl.BlockSpec(memory_space=pl.ANY)] * 3 + [full] * 3
+    return grad_call(last_kernel, ids, pair, carried, specs, outs, [half] * 6, scratch)
+
+
+def newton_kernel(ids, own_ref, other_ref, w_ref, u_ref, g_ref):
+    half = own_ref.shape[0]
+    g_ref[pl.ds(pl.multiple_of(ids[1] * half, 16), half), :] = own_ref[...]
+    g_ref[pl.ds(pl.multiple_of((1 - ids[1]) * half, 16), half), :] = other_ref[...]
     grad = g_ref[...].astype(f32)
     total = jnp.sqrt(jnp.sum(grad * grad))
     x = (grad / (total + frob_eps)).astype(bf16)
@@ -219,21 +231,23 @@
     u_ref[...] = (w_ref[0] + step_size * x.astype(f32)).astype(bf16)
 
 
-def updated(ids, grad, weight):
-    width = grad.shape[0]
+def updated(ids, halves, weight):
+    rows, width = halves[0].shape
+    half = pl.BlockSpec((rows, width), lambda i, ids: (0, 0))
     full = pl.BlockSpec((width, width), lambda i, ids: (0, 0))
     return pl.pallas_call(
         newton_kernel,
         grid_spec=pltpu.PrefetchScalarGridSpec(
             num_scalar_prefetch=1,
             grid=(1,),
-            in_specs=[full, pl.BlockSpec((1, width, width), lambda i, ids: (ids[0], 0, 0))],
+            in_specs=[half, half, pl.BlockSpec((1, width, width), lambda i, ids: (ids[0], 0, 0))],
             out_specs=full,
+            scratch_shapes=[pltpu.VMEM((width, width), bf16)],
         ),
         out_shape=jax.ShapeDtypeStruct((width, width), bf16),
         cost_estimate=cost(12 * width**3, 8 * width * width),
         compiler_params=pltpu.CompilerParams(vmem_limit_bytes=60 << 20),
-    )(ids, grad, weight)
+    )(ids, *halves, weight)
 
 
 def gate_kernel(q_ref, u1_ref, u3_ref, f_ref):
@@ -271,20 +285,23 @@
         keep = keep + came.astype(f32)
         if place + 1 == len(steps):
             whole = keep.astype(bf16)
-            break
-        axis, size, bit = steps[place + 1]
-        rows = keep.shape[0] // 2
-        side = (lax.axis_index(axis) >> bit) & 1
-        send = lax.dynamic_slice_in_dim(keep, (1 - side) * rows, rows, 0).astype(bf16)
-        keep = lax.dynamic_slice_in_dim(keep, side * rows, rows, 0)
-    for place, (axis, size, bit) in reversed(list(enumerate(steps))):
+        elif place + 2 == len(steps):
+            send = keep.astype(bf16)
+        else:
+            axis, size, bit = steps[place + 1]
+            rows = keep.shape[0] // 2
+            side = (lax.axis_index(axis) >> bit) & 1
+            send = lax.dynamic_slice_in_dim(keep, (1 - side) * rows, rows, 0).astype(bf16)
+            keep = lax.dynamic_slice_in_dim(keep, side * rows, rows, 0)
+    for place, (axis, size, bit) in reversed(list(enumerate(steps[:-1]))):
         pairs = [(i, i ^ (1 << bit)) for i in range(size)]
         other = lax.ppermute(whole, axis, pairs)
+        if place == 0:
+            return whole, other
         first = ((lax.axis_index(axis) >> bit) & 1) == 0
         whole = jnp.concatenate(
             [jnp.where(first, whole, other), jnp.where(first, other, whole)], axis=0
         )
-    return whole
 
 
 def per_device(
@@ -334,7 +351,7 @@
         sizes = {"l2": min(lo, 2), "h2": min(hi, 2)}
         sizes["l1"] = lo // sizes["l2"]
         sizes["h1"] = hi // sizes["h2"]
-        assert hi > 1 and hi * lo == ctx and ctx & (ctx - 1) == 0
+        assert hi > 2 and hi * lo == ctx and ctx & (ctx - 1) == 0
         assert w_first.shape[1] % (2 * hi) == 0
         order = ("h1", "l1", "h2", "l2")
         shape = [head] + [sizes[axis] for axis in order]

time: 280 us -> 263 us (0.939)
  starting transfers between devices: 41.4 us -> 29.7 us
  other arithmetic: 6.84 us -> 3.58 us
    ppermute x6 -> x3, waiting for transfers between devices: 40.1 us -> 0.01 us  [summed(): other = lax.ppermute(whole, axis, pairs)]
    ppermute x6, waiting for transfers between devices: 21.7 us -> 51.4 us  [summed(): came = lax.ppermute(send, axis, pairs)]
    ppermute x6 -> x3, starting transfers between devices: 15.2 us -> 4.75 us  [summed(): other = lax.ppermute(whole, axis, pairs)]
    all_to_all x2, waiting for transfers between devices: 43.8 us -> 54.1 us  [per_device(): pairs.append(exchange(pair))]
    concatenate x6 -> x0, other arithmetic: 3.08 us -> none  [summed(): jnp.concatenate([jnp.where(first, whole, other), jnp.where(first, other,...]
  transfers between devices with their start and end apart: 15 -> 12, of which waited for: 14 -> 8; matrix products, arithmetic and copies ran while one was open for 2% -> 1% of each run, Pallas kernels for 18% -> 23%
where the time goes in v2:
time: 263 us; the launch traced here: 262 us
  waiting for transfers between devices  106 us (40%)
  Pallas kernels  82.9 us (32%)
  blocking collectives  36.6 us (14%)
  starting transfers between devices  29.7 us (11%)
  local copies, waits for them, and re-layouts  3.97 us (2%)
  other arithmetic  3.58 us (1%)
    all_to_all x2, waiting for transfers between devices, per_device(): pairs.append(exchange(pair))  54.1 us
    ppermute x6, waiting for transfers between devices, summed(): came = lax.ppermute(send, axis, pairs)  51.4 us
    all_to_all x1, blocking collectives, per_device(): return back_to_columns(exchange(normed.reshape(heads, -1, width)))  36.6 us
    pallas_call x2, Pallas kernels, grad_call(): pl.pallas_call(kernel, grid_spec=pltpu.PrefetchScalarGridSpec(num_scalar_...  26.4 us
    pallas_call x3, Pallas kernels, updated(): pl.pallas_call(newton_kernel, grid_spec=pltpu.PrefetchScalarGridSpec(num_...  25.4 us
    pallas_call x2, Pallas kernels, over_tokens(): pl.pallas_call(kernel, grid=(tokens // block,), in_specs=[tile] + [full]...  14 us
    ppermute x6, starting transfers between devices, summed(): came = lax.ppermute(send, axis, pairs)  11.6 us
    all_to_all x2, starting transfers between devices, per_device(): pairs.append(exchange(pair))  9.79 us
  transfers between devices with their start and end apart: 12, of which 8 were waited for; matrix products, arithmetic and copies ran while one was open for 1% of the time, Pallas kernels for 23%

profile of v2, /device:TPU:0, one launch (start us, length us, event | category | flops | bytes accessed | tf_op | source)
XLA Modules:
  0.0 262.4 jit_solution(4725849598983521090)
XLA Ops:
  1.4 2.8 %shard_map.92 = bf16[8,2,64,640]{3,2,1,0:T(8,128)(2,1)} custom-call(bf16[256,5120]{1,0:T(8,128)(2,1)} %k_ref.3, bf16[256,5120]{1,0:T(8,128)(2,1)} %v_ref.3, bf16[256,8]{1,0:T(8,128)(2,1)} %copy.10.rate_ref, f32[1,5120]{1,0:T(1,128)} %bitcast.8), custom_call_target="tpu_custom_call" | custom-call | flops 3932160 | bytes 2621440 | tf_op jit(solution)/shard_map/pallas_call | solution.py:80
  4.2 5.3 %all-to-all-start.1 = ((bf16[8,2,64,640]{3,2,1,0:T(8,128)(2,1)}), bf16[8,2,64,640]{3,2,1,0:T(8,128)(2,1)S(1)}, u32[]{:S(2)}, u32[]{:S(2)}) async-start(bf16[8,2,64,640]{3,2,1,0:T(8,128)(2,1)} %shard_map.92), calls=%async_computation.1 | async-start | bytes 2621440 | tf_op jit(solution)/shard_map/all_to_all | solution.py:329
  9.5 5.8 %shard_map.93 = bf16[8,2,192,640]{3,2,1,0:T(8,128)(2,1)} custom-call(bf16[256,5120]{1,0:T(8,128)(2,1)} %k_ref.3, bf16[256,5120]{1,0:T(8,128)(2,1)} %v_ref.3, bf16[256,8]{1,0:T(8,128)(2,1)} %copy.10.rate_ref, f32[1,5120]{1,0:T(1,128)} %bitcast.9), custom_call_target="tpu_custom_call" | custom-call | flops 11796480 | bytes 7864320 | tf_op jit(solution)/shard_map/pallas_call | solution.py:80
  15.2 12.4 %all-to-all-done.1.pair_ref = bf16[8,2,64,640]{3,2,1,0:T(8,128)(2,1)S(1)} async-done(((bf16[8,2,64,640]{3,2,1,0:T(8,128)(2,1)}), bf16[8,2,64,640]{3,2,1,0:T(8,128)(2,1)S(1)}, u32[]{:S(2)}, u32[]{:S(2)}) %all-to-all-start.1) | async-done | bytes 1310752 | tf_op jit(solution)/shard_map/all_to_all | solution.py:329
  28.7 4.5 %all-to-all-start.2 = ((bf16[8,2,192,640]{3,2,1,0:T(8,128)(2,1)}), bf16[8,2,192,640]{3,2,1,0:T(8,128)(2,1)}, u32[]{:S(2)}, u32[]{:S(2)}) async-start(bf16[8,2,192,640]{3,2,1,0:T(8,128)(2,1)} %shard_map.93), calls=%async_computation.2 | async-start | bytes 7864320 | tf_op jit(solution)/shard_map/all_to_all | solution.py:329
  33.2 4.6 %shard_map.91 = bf16[8,256,640]{2,1,0:T(8,128)(2,1)} custom-call(bf16[256,5120]{1,0:T(8,128)(2,1)} %x_ref.1, f32[1,5120]{1,0:T(1,128)} %bitcast.10), custom_call_target="tpu_custom_call" | custom-call | flops 10485760 | bytes 5242880 | tf_op jit(solution)/shard_map/pallas_call | solution.py:61
  37.8 41.7 %all-to-all-done.2.pair_ref = bf16[8,2,192,640]{3,2,1,0:T(8,128)(2,1)} async-done(((bf16[8,2,192,640]{3,2,1,0:T(8,128)(2,1)}), bf16[8,2,192,640]{3,2,1,0:T(8,128)(2,1)}, u32[]{:S(2)}, u32[]{:S(2)}) %all-to-all-start.2) | async-done | bytes 3932192 | tf_op jit(solution)/shard_map/all_to_all | solution.py:329
  79.5 3.6 %all-to-all-start = ((bf16[8,256,640]{2,1,0:T(8,128)(2,1)}), bf16[8,256,640]{2,1,0:T(8,128)(2,1)S(1)}, u32[]{:S(2)}, u32[]{:S(2)}) async-start(bf16[8,256,640]{2,1,0:T(8,128)(2,1)} %shard_map.91), calls=%async_computation | async-start | bytes 5242880 | tf_op jit(solution)/shard_map/all_to_all | solution.py:331
  83.8 17.1 %shard_map.94 = (f32[640,640]{1,0:T(8,128)}, f32[640,640]{1,0:T(8,128)}, f32[640,640]{1,0:T(8,128)}, bf16[640,640]{1,0:T(8,128)(2,1)}, bf16[640,640]{1,0:T(8,128)(2,1)}, /*index=5*/bf16[640,640]{1,0:T(8,128)(2,1)}) custom-call(s32[2]{0:T(128)} %pad_add_fusion.ids, bf16[8,2,192,640]{3,2,1,0:T(8,128)(2,1)} %all-to-all-done.2.pair_ref, f32[4,640,640]{2,1,0:T(8,128)} %w_ref.3, ...), custom_call_target="tpu_custom_call" | custom-call | flops 7549747200 | bytes 3932160 | tf_op jit(solution)/shard_map/pallas_call | solution.py:181
  100.9 9.2 %shard_map.95 = (bf16[320,640]{1,0:T(8,128)(2,1)}, f32[320,640]{1,0:T(8,128)}, bf16[320,640]{1,0:T(8,128)(2,1)}, f32[320,640]{1,0:T(8,128)}, bf16[320,640]{1,0:T(8,128)(2,1)}, /*index=5*/f32[320,640]{1,0:T(8,128)}) custom-call(s32[2]{0:T(128)} %pad_add_fusion.ids, bf16[8,2,64,640]{3,2,1,0:T(8,128)(2,1)} %copy-done.4, f32[640,640]{1,0:T(8,128)} %get-tuple-element.17.was1, ...), custom_call_target="tpu_custom_call" | custom-call | flops 2516582400 | bytes 1310720 | tf_op jit(solution)/shard_map/pallas_call | solution.py:181
  110.2 1.6 collective-permute-start.3
  112.3 1.5 collective-permute-start.6
  113.8 9.0 %collective-permute-done.3 = bf16[320,640]{1,0:T(8,128)(2,1)S(1)} collective-permute-done((bf16[320,640]{1,0:T(8,128)(2,1)}, bf16[320,640]{1,0:T(8,128)(2,1)S(1)}, u32[]{:S(2)}, u32[]{:S(2)}) %collective-permute-start.3) | collective-permute-done | bytes 409632 | tf_op jit(solution)/shard_map/ppermute | solution.py:284
  124.0 2.7 %collective-permute-start.4 = (bf16[320,640]{1,0:T(8,128)(2,1)S(1)}, bf16[320,640]{1,0:T(8,128)(2,1)S(1)}, u32[]{:S(2)}, u32[]{:S(2)}) collective-permute-start(bf16[320,640]{1,0:T(8,128)(2,1)S(1)} %fusion.1), channel_id=1, source_target_pairs={{0,8},{8,0},{1,9},{9,1},{2,10},{10,2},{3,11},{11,3},{4,12},{12,4},... | collective-permute-start | bytes 1228808 | tf_op jit(solution)/shard_map/ppermute | solution.py:284
  126.7 4.9 %collective-permute-done = bf16[320,640]{1,0:T(8,128)(2,1)S(1)} collective-permute-done((bf16[320,640]{1,0:T(8,128)(2,1)}, bf16[320,640]{1,0:T(8,128)(2,1)S(1)}, u32[]{:S(2)}, u32[]{:S(2)}) %collective-permute-start) | collective-permute-done | bytes 409632 | tf_op jit(solution)/shard_map/ppermute | solution.py:284
  132.9 2.7 %collective-permute-start.1 = (bf16[320,640]{1,0:T(8,128)(2,1)S(1)}, bf16[320,640]{1,0:T(8,128)(2,1)S(1)}, u32[]{:S(2)}, u32[]{:S(2)}) collective-permute-start(bf16[320,640]{1,0:T(8,128)(2,1)S(1)} %fusion), channel_id=1, source_target_pairs={{0,8},{8,0},{1,9},{9,1},{2,10},{10,2},{3,11},{11,3},{4,12},{12,4},... | collective-permute-start | bytes 1228808 | tf_op jit(solution)/shard_map/ppermute | solution.py:284
  135.5 4.2 %collective-permute-done.6 = bf16[320,640]{1,0:T(8,128)(2,1)S(1)} collective-permute-done((bf16[320,640]{1,0:T(8,128)(2,1)}, bf16[320,640]{1,0:T(8,128)(2,1)S(1)}, u32[]{:S(2)}, u32[]{:S(2)}) %collective-permute-start.6) | collective-permute-done | bytes 409632 | tf_op jit(solution)/shard_map/ppermute | solution.py:284
  139.9 2.7 %collective-permute-start.7 = (bf16[320,640]{1,0:T(8,128)(2,1)S(1)}, bf16[320,640]{1,0:T(8,128)(2,1)S(1)}, u32[]{:S(2)}, u32[]{:S(2)}) collective-permute-start(bf16[320,640]{1,0:T(8,128)(2,1)S(1)} %fusion.2), channel_id=1, source_target_pairs={{0,8},{8,0},{1,9},{9,1},{2,10},{10,2},{3,11},{11,3},{4,12},{12,4},... | collective-permute-start | bytes 1228808 | tf_op jit(solution)/shard_map/ppermute | solution.py:284
  142.5 20.0 %collective-permute-done.4 = bf16[320,640]{1,0:T(8,128)(2,1)S(1)} collective-permute-done((bf16[320,640]{1,0:T(8,128)(2,1)S(1)}, bf16[320,640]{1,0:T(8,128)(2,1)S(1)}, u32[]{:S(2)}, u32[]{:S(2)}) %collective-permute-start.4) | collective-permute-done | bytes 409632 | tf_op jit(solution)/shard_map/ppermute | solution.py:284
  162.7 1.6 collective-permute-start.5
  164.3 7.1 %collective-permute-done.1 = bf16[320,640]{1,0:T(8,128)(2,1)S(1)} collective-permute-done((bf16[320,640]{1,0:T(8,128)(2,1)S(1)}, bf16[320,640]{1,0:T(8,128)(2,1)S(1)}, u32[]{:S(2)}, u32[]{:S(2)}) %collective-permute-start.1) | collective-permute-done | bytes 409632 | tf_op jit(solution)/shard_map/ppermute | solution.py:284
  171.5 1.6 collective-permute-start.2
  173.1 6.2 %collective-permute-done.7 = bf16[320,640]{1,0:T(8,128)(2,1)S(1)} collective-permute-done((bf16[320,640]{1,0:T(8,128)(2,1)S(1)}, bf16[320,640]{1,0:T(8,128)(2,1)S(1)}, u32[]{:S(2)}, u32[]{:S(2)}) %collective-permute-start.7) | collective-permute-done | bytes 409632 | tf_op jit(solution)/shard_map/ppermute | solution.py:284
  179.4 1.6 collective-permute-start.8
  181.0 8.5 %shard_map.97.u3_ref = bf16[640,640]{1,0:T(8,128)(2,1)} custom-call(s32[2]{0:T(128)} %pad_add_fusion.ids, bf16[320,640]{1,0:T(8,128)(2,1)} %copy-done.5, bf16[320,640]{1,0:T(8,128)(2,1)} %collective-permute-done.5.other_ref, f32[4,640,640]{2,1,0:T(8,128)} %w_ref.4), custom_call_target="tpu_custom_call" | custom-call | flops 3145728000 | bytes 3276800 | tf_op jit(solution)/shard_map/pallas_call | solution.py:238
  189.4 8.5 %shard_map.96.u1_ref = bf16[640,640]{1,0:T(8,128)(2,1)} custom-call(s32[2]{0:T(128)} %pad_add_fusion.ids, bf16[320,640]{1,0:T(8,128)(2,1)} %copy-done.7, bf16[320,640]{1,0:T(8,128)(2,1)} %collective-permute-done.2.other_ref, f32[4,640,640]{2,1,0:T(8,128)} %w_ref.3), custom_call_target="tpu_custom_call" | custom-call | flops 3145728000 | bytes 3276800 | tf_op jit(solution)/shard_map/pallas_call | solution.py:238
  197.9 1.5 copy-done.3
  199.4 7.8 %shard_map.98.f_ref = bf16[2048,640]{1,0:T(8,128)(2,1)} custom-call(bf16[2048,640]{1,0:T(8,128)(2,1)} %bitcast.6, bf16[640,640]{1,0:T(8,128)(2,1)} %shard_map.96.u1_ref, bf16[640,640]{1,0:T(8,128)(2,1)} %shard_map.97.u3_ref), custom_call_target="tpu_custom_call" | custom-call | flops 3355443200 | bytes 5242880 | tf_op jit(solution)/shard_map/pallas_call | solution.py:270
  207.2 8.5 %shard_map.99.u2_ref = bf16[640,640]{1,0:T(8,128)(2,1)} custom-call(s32[2]{0:T(128)} %pad_add_fusion.ids, bf16[320,640]{1,0:T(8,128)(2,1)} %copy-done.6, bf16[320,640]{1,0:T(8,128)(2,1)} %collective-permute-done.8.other_ref, f32[4,640,640]{2,1,0:T(8,128)} %w_ref.5), custom_call_target="tpu_custom_call" | custom-call | flops 3145728000 | bytes 3276800 | tf_op jit(solution)/shard_map/pallas_call | solution.py:238
  215.7 6.2 %shard_map.100 = bf16[2048,640]{1,0:T(8,128)(2,1)} custom-call(bf16[2048,640]{1,0:T(8,128)(2,1)} %shard_map.98.f_ref, bf16[640,640]{1,0:T(8,128)(2,1)} %shard_map.99.u2_ref), custom_call_target="tpu_custom_call" | custom-call | flops 1677721600 | bytes 5242880 | tf_op jit(solution)/shard_map/pallas_call | solution.py:270
  221.9 36.6 %all_to_all.20.x_ref = bf16[8,256,640]{2,1,0:T(8,128)(2,1)} all-to-all(bf16[8,256,640]{2,1,0:T(8,128)(2,1)} %bitcast.7), channel_id=1, replica_groups=mesh['head'=2,'h1'=2,'l1'=2,'h2'=2,'l2'=2] {'head','l1','l2'}, dimensions={0} | all-to-all | bytes 5242880 | tf_op jit(solution)/shard_map/all_to_all | solution.py:342
  258.4 4.0 %shard_map.101 = bf16[256,5120]{1,0:T(8,128)(2,1)} custom-call(bf16[8,256,640]{2,1,0:T(8,128)(2,1)} %all_to_all.20.x_ref), custom_call_target="tpu_custom_call" | custom-call | flops 1310720 | bytes 5242880 | tf_op jit(solution)/shard_map/pallas_call | solution.py:103
  (28 shorter events, 6.6 us)
Async XLA Ops:
  4.2 23.4 %all-to-all-start.1 = ((bf16[8,2,64,640]{3,2,1,0:T(8,128)(2,1)}), bf16[8,2,64,640]{3,2,1,0:T(8,128)(2,1)S(1)}, u32[]{:S(2)}, u32[]{:S(2)}) async-start(bf16[8,2,64,640]{3,2,1,0:T(8,128)(2,1)} %shard_map.92), calls=%async_computation.1 | async-start | bytes 2621440 | tf_op jit(solution)/shard_map/all_to_all | solution.py:329
  27.6 1.0 copy-start.4
  28.7 50.8 %all-to-all-start.2 = ((bf16[8,2,192,640]{3,2,1,0:T(8,128)(2,1)}), bf16[8,2,192,640]{3,2,1,0:T(8,128)(2,1)}, u32[]{:S(2)}, u32[]{:S(2)}) async-start(bf16[8,2,192,640]{3,2,1,0:T(8,128)(2,1)} %shard_map.93), calls=%async_computation.2 | async-start | bytes 7864320 | tf_op jit(solution)/shard_map/all_to_all | solution.py:329
  79.5 118.4 %all-to-all-start = ((bf16[8,256,640]{2,1,0:T(8,128)(2,1)}), bf16[8,256,640]{2,1,0:T(8,128)(2,1)S(1)}, u32[]{:S(2)}, u32[]{:S(2)}) async-start(bf16[8,256,640]{2,1,0:T(8,128)(2,1)} %shard_map.91), calls=%async_computation | async-start | bytes 5242880 | tf_op jit(solution)/shard_map/all_to_all | solution.py:331
  110.2 29.6 %copy-start = (f32[320,640]{1,0:T(8,128)S(1)}, f32[320,640]{1,0:T(8,128)}, u32[]{:S(2)}) copy-start(f32[320,640]{1,0:T(8,128)} %get-tuple-element.27) | copy-start | bytes 2457604
  110.2 52.4 %copy-start.2 = (f32[320,640]{1,0:T(8,128)S(1)}, f32[320,640]{1,0:T(8,128)}, u32[]{:S(2)}) copy-start(f32[320,640]{1,0:T(8,128)} %get-tuple-element.25) | copy-start | bytes 2457604
  110.2 12.6 %collective-permute-start.3 = (bf16[320,640]{1,0:T(8,128)(2,1)}, bf16[320,640]{1,0:T(8,128)(2,1)S(1)}, u32[]{:S(2)}, u32[]{:S(2)}) collective-permute-start(bf16[320,640]{1,0:T(8,128)(2,1)} %get-tuple-element.26), channel_id=1, source_target_pairs={{0,2},{2,0},{1,3},{3,1},{4,6},{6,4},{5,7},{7,5},{8,10},{10,8},{9,1... | collective-permute-start | bytes 1228808 | tf_op jit(solution)/shard_map/ppermute | solution.py:284
  111.8 19.8 %collective-permute-start = (bf16[320,640]{1,0:T(8,128)(2,1)}, bf16[320,640]{1,0:T(8,128)(2,1)S(1)}, u32[]{:S(2)}, u32[]{:S(2)}) collective-permute-start(bf16[320,640]{1,0:T(8,128)(2,1)} %get-tuple-element.24), channel_id=1, source_target_pairs={{0,2},{2,0},{1,3},{3,1},{4,6},{6,4},{5,7},{7,5},{8,10},{10,8},{9,1... | collective-permute-start | bytes 1228808 | tf_op jit(solution)/shard_map/ppermute | solution.py:284
  112.3 27.5 %collective-permute-start.6 = (bf16[320,640]{1,0:T(8,128)(2,1)}, bf16[320,640]{1,0:T(8,128)(2,1)S(1)}, u32[]{:S(2)}, u32[]{:S(2)}) collective-permute-start(bf16[320,640]{1,0:T(8,128)(2,1)} %get-tuple-element.28), channel_id=1, source_target_pairs={{0,2},{2,0},{1,3},{3,1},{4,6},{6,4},{5,7},{7,5},{8,10},{10,8},{9,1... | collective-permute-start | bytes 1228808 | tf_op jit(solution)/shard_map/ppermute | solution.py:284
  124.0 38.5 %collective-permute-start.4 = (bf16[320,640]{1,0:T(8,128)(2,1)S(1)}, bf16[320,640]{1,0:T(8,128)(2,1)S(1)}, u32[]{:S(2)}, u32[]{:S(2)}) collective-permute-start(bf16[320,640]{1,0:T(8,128)(2,1)S(1)} %fusion.1), channel_id=1, source_target_pairs={{0,8},{8,0},{1,9},{9,1},{2,10},{10,2},{3,11},{11,3},{4,12},{12,4},... | collective-permute-start | bytes 1228808 | tf_op jit(solution)/shard_map/ppermute | solution.py:284
  131.6 39.8 %copy-start.1 = (f32[320,640]{1,0:T(8,128)S(1)}, f32[320,640]{1,0:T(8,128)}, u32[]{:S(2)}) copy-start(f32[320,640]{1,0:T(8,128)} %get-tuple-element.23) | copy-start | bytes 2457604
  132.9 38.5 %collective-permute-start.1 = (bf16[320,640]{1,0:T(8,128)(2,1)S(1)}, bf16[320,640]{1,0:T(8,128)(2,1)S(1)}, u32[]{:S(2)}, u32[]{:S(2)}) collective-permute-start(bf16[320,640]{1,0:T(8,128)(2,1)S(1)} %fusion), channel_id=1, source_target_pairs={{0,8},{8,0},{1,9},{9,1},{2,10},{10,2},{3,11},{11,3},{4,12},{12,4},... | collective-permute-start | bytes 1228808 | tf_op jit(solution)/shard_map/ppermute | solution.py:284
  139.9 39.3 %collective-permute-start.7 = (bf16[320,640]{1,0:T(8,128)(2,1)S(1)}, bf16[320,640]{1,0:T(8,128)(2,1)S(1)}, u32[]{:S(2)}, u32[]{:S(2)}) collective-permute-start(bf16[320,640]{1,0:T(8,128)(2,1)S(1)} %fusion.2), channel_id=1, source_target_pairs={{0,8},{8,0},{1,9},{9,1},{2,10},{10,2},{3,11},{11,3},{4,12},{12,4},... | collective-permute-start | bytes 1228808 | tf_op jit(solution)/shard_map/ppermute | solution.py:284
  162.7 18.3 %copy-start.5 = (bf16[320,640]{1,0:T(8,128)(2,1)}, bf16[320,640]{1,0:T(8,128)(2,1)S(1)}, u32[]{:S(2)}) copy-start(bf16[320,640]{1,0:T(8,128)(2,1)S(1)} %add_convert_fusion.1.own_ref) | copy-start | bytes 1228804
  162.7 18.2 %collective-permute-start.5 = (bf16[320,640]{1,0:T(8,128)(2,1)S(1)}, bf16[320,640]{1,0:T(8,128)(2,1)}, u32[]{:S(2)}, u32[]{:S(2)}) collective-permute-start(bf16[320,640]{1,0:T(8,128)(2,1)S(1)} %add_convert_fusion.1.own_ref), channel_id=1, source_target_pairs={{0,2},{2,0},{1,3},{3,1},{4,6},{6,4},{5,7},{7,5},{8,10},{10,8},{9,1... | collective-permute-start | bytes 1228808 | tf_op jit(solution)/shard_map/ppermute | solution.py:298
  171.5 18.0 %copy-start.7 = (bf16[320,640]{1,0:T(8,128)(2,1)}, bf16[320,640]{1,0:T(8,128)(2,1)S(1)}, u32[]{:S(2)}) copy-start(bf16[320,640]{1,0:T(8,128)(2,1)S(1)} %add_convert_fusion.2.own_ref) | copy-start | bytes 1228804
  171.5 18.0 %collective-permute-start.2 = (bf16[320,640]{1,0:T(8,128)(2,1)S(1)}, bf16[320,640]{1,0:T(8,128)(2,1)}, u32[]{:S(2)}, u32[]{:S(2)}) collective-permute-start(bf16[320,640]{1,0:T(8,128)(2,1)S(1)} %add_convert_fusion.2.own_ref), channel_id=1, source_target_pairs={{0,2},{2,0},{1,3},{3,1},{4,6},{6,4},{5,7},{7,5},{8,10},{10,8},{9,1... | collective-permute-start | bytes 1228808 | tf_op jit(solution)/shard_map/ppermute | solution.py:298
  179.4 10.1 %copy-start.6 = (bf16[320,640]{1,0:T(8,128)(2,1)}, bf16[320,640]{1,0:T(8,128)(2,1)S(1)}, u32[]{:S(2)}) copy-start(bf16[320,640]{1,0:T(8,128)(2,1)S(1)} %add_convert_fusion.own_ref) | copy-start | bytes 1228804
  179.4 27.8 %collective-permute-start.8 = (bf16[320,640]{1,0:T(8,128)(2,1)S(1)}, bf16[320,640]{1,0:T(8,128)(2,1)}, u32[]{:S(2)}, u32[]{:S(2)}) collective-permute-start(bf16[320,640]{1,0:T(8,128)(2,1)S(1)} %add_convert_fusion.own_ref), channel_id=1, source_target_pairs={{0,2},{2,0},{1,3},{3,1},{4,6},{6,4},{5,7},{7,5},{8,10},{10,8},{9,1... | collective-permute-start | bytes 1228808 | tf_op jit(solution)/shard_map/ppermute | solution.py:298
  197.9 1.5 copy-start.3

commit v3 on v2

--- a/solution.py
+++ b/solution.py
@@ -45,13 +45,18 @@
     normalized(x_ref, gain_ref, out_ref, lambda head: head)
 
 
-def pair_kernel(k_ref, v_ref, rate_ref, gain_ref, out_ref):
-    heads, width = out_ref.shape[0], out_ref.shape[-1]
-    normalized(k_ref, gain_ref, out_ref, lambda head: (head, 0))
-    for head in range(heads):
-        cols = slice(head * width, (head + 1) * width)
-        rate = rate_ref[:, head : head + 1].astype(f32)
-        out_ref[head, 1] = (v_ref[:, cols].astype(f32) * rate).astype(bf16)
+def pair_kernel(ids, k_ref, v_ref, rate_ref, gain_ref, *out_refs):
+    width = out_refs[0].shape[-1]
+    wide = k_ref[...].astype(f32)
+    factor = lax.rsqrt(jnp.mean(wide * wide, axis=-1, keepdims=True) + epsilon)
+    rates = rate_ref[...].astype(f32)
+    lane = lax.broadcasted_iota(jnp.int32, rates.shape, 1)
+    for k, out_ref in enumerate(out_refs):
+        head = ids[2] ^ k
+        cols = pl.ds(pl.multiple_of(head * width, 128), width)
+        out_ref[0] = (k_ref[:, cols].astype(f32) * factor * gain_ref[:, cols]).astype(bf16)
+        rate = jnp.sum(jnp.where(lane == head, rates, 0.0), axis=1, keepdims=True)
+        out_ref[1] = (v_ref[:, cols].astype(f32) * rate).astype(bf16)
 
 
 def prepared_queries(x, gain, heads):
@@ -71,49 +76,80 @@
     )(x, gain)
 
 
-def prepared_pair(keys, values, rates, gain, first, steps, block):
+def prepared_pair(ids, keys, values, rates, gain, first, steps, block):
     heads = rates.shape[1]
     model = keys.shape[1]
     rows = block * steps
     width = model // heads
-    tile = pl.BlockSpec((block, model), lambda i: (first + i, 0))
+    tile = pl.BlockSpec((block, model), lambda i, ids: (first + i, 0))
     return pl.pallas_call(
         pair_kernel,
-        grid=(steps,),
-        in_specs=[
-            tile,
-            tile,
-            pl.BlockSpec((block, heads), lambda i: (first + i, 0)),
-            pl.BlockSpec((1, model), lambda i: (0, 0)),
-        ],
-        out_specs=pl.BlockSpec((heads, 2, block, width), lambda i: (0, 0, i, 0)),
-        out_shape=jax.ShapeDtypeStruct((heads, 2, rows, width), bf16),
+        grid_spec=pltpu.PrefetchScalarGridSpec(
+            num_scalar_prefetch=1,
+            grid=(steps,),
+            in_specs=[
+                tile,
+                tile,
+                pl.BlockSpec((block, heads), lambda i, ids: (first + i, 0)),
+                pl.BlockSpec((1, model), lambda i, ids: (0, 0)),
+            ],
+            out_specs=[pl.BlockSpec((2, block, width), lambda i, ids: (0, i, 0))] * heads,
+        ),
+        out_shape=[jax.ShapeDtypeStruct((2, rows, width), bf16)] * heads,
         cost_estimate=cost(12 * rows * model, 8 * rows * model),
-    )(keys, values, rates, gain)
-
-
-def back_to_columns(x):
-    heads, rows, width = x.shape
-
-    def kernel(x_ref, out_ref):
-        for head in range(heads):
-            out_ref[:, head * width : (head + 1) * width] = x_ref[head]
-
-    block = rows // 4 if rows % 64 == 0 else rows
+    )(ids, keys, values, rates, gain)
+
+
+def back_to_columns(ids, blocks):
+    rows, width = blocks[0].shape
+    heads = len(blocks)
+
+    def kernel(ids, *refs):
+        out_ref = refs[-1]
+        for k, ref in enumerate(refs[:-1]):
+            start = pl.multiple_of((ids[2] ^ k) * width, 128)
+            out_ref[:, pl.ds(start, width)] = ref[...]
+
+    block = rows // 4
     return pl.pallas_call(
         kernel,
-        grid=(rows // block,),
-        in_specs=[pl.BlockSpec((heads, block, width), lambda i: (0, i, 0))],
-        out_specs=pl.BlockSpec((block, heads * width), lambda i: (i, 0)),
+        grid_spec=pltpu.PrefetchScalarGridSpec(
+            num_scalar_prefetch=1,
+            grid=(rows // block,),
+            in_specs=[pl.BlockSpec((block, width), lambda i, ids: (i, 0))] * heads,
+            out_specs=pl.BlockSpec((block, heads * width), lambda i, ids: (i, 0)),
+        ),
         out_shape=jax.ShapeDtypeStruct((rows, heads * width), bf16),
         cost_estimate=cost(rows * heads * width, 4 * rows * heads * width),
-    )(x)
-
-
-def accumulate(pair_ref, wb1, wb2, wb3, acc1, acc2, acc3):
-    sources, _, rows, width = pair_ref.shape
-    keys = pair_ref[:, 0].reshape(sources * rows, width)
-    scaled = pair_ref[:, 1].reshape(sources * rows, width)
+    )(ids, *blocks)
+
+
+def fetch(pair_refs, buffer, sems):
+    loads = [
+        pltpu.make_async_copy(ref, buffer.at[i], sems.at[i]) for i, ref in enumerate(pair_refs)
+    ]
+    half = len(loads) // 2
+
+    @pl.when(pl.program_id(0) == 0)
+    def _():
+        for load in loads:
+            load.start()
+
+    return loads[:half], loads[half:]
+
+
+def accumulate(groups, buffer, wb1, wb2, wb3, acc1, acc2, acc3):
+    for step, group in enumerate(groups):
+
+        @pl.when(pl.program_id(0) == step)
+        def _():
+            for load in group:
+                load.wait()
+
+    sources, rows, width = buffer.shape[0] // 2, buffer.shape[2], buffer.shape[3]
+    now = pl.ds(pl.program_id(0) * sources, sources)
+    keys = buffer[now, 0].reshape(sources * rows, width)
+    scaled = buffer[now, 1].reshape(sources * rows, width)
     pre1 = mm(keys, wb1[...])
     pre3 = mm(keys, wb3[...])
     sigmoid = jax.nn.sigmoid(pre1)
@@ -128,9 +164,10 @@
     acc2[...] += mm(hidden.T, scaled)
 
 
-def first_kernel(
-    ids, pair_ref, w1_ref, w2_ref, w3_ref, acc1, acc2, acc3, wb1, wb2, wb3
-):
+def first_kernel(heads, ids, *refs):
+    w1_ref, w2_ref, w3_ref, acc1, acc2, acc3, wb1, wb2, wb3, buffer, pair_sems = refs[heads:]
+    groups = fetch(refs[:heads], buffer, pair_sems)
+
     @pl.when(pl.program_id(0) == 0)
     def _():
         wb1[...] = w1_ref[0].astype(bf16)
@@ -139,13 +176,15 @@
         for acc in (acc1, acc2, acc3):
             acc[...] = jnp.zeros_like(acc)
 
-    accumulate(pair_ref, wb1, wb2, wb3, acc1, acc2, acc3)
-
-
-def last_kernel(
-    ids, pair_ref, was1, was2, was3, wb1, wb2, wb3,
-    send1, keep1, send2, keep2, send3, keep3, acc1, acc2, acc3, old1, old2, old3, sems,
-):
+    accumulate(groups, buffer, wb1, wb2, wb3, acc1, acc2, acc3)
+
+
+def last_kernel(heads, ids, *refs):
+    was1, was2, was3, wb1, wb2, wb3, send1, keep1, send2, keep2, send3, keep3 = refs[
+        heads : heads + 12
+    ]
+    acc1, acc2, acc3, old1, old2, old3, sems, buffer, pair_sems = refs[heads + 12 :]
+    groups = fetch(refs[:heads], buffer, pair_sems)
     loads = [
         pltpu.make_async_copy(was, old, sems.at[i])
         for i, (was, old) in enumerate(((was1, old1), (was2, old2), (was3, old3)))
@@ -158,7 +197,7 @@
         for acc in (acc1, acc2, acc3):
             acc[...] = jnp.zeros_like(acc)
 
-    accumulate(pair_ref, wb1, wb2, wb3, acc1, acc2, acc3)
+    accumulate(groups, buffer, wb1, wb2, wb3, acc1, acc2, acc3)
 
     @pl.when(pl.program_id(0) == pl.num_programs(0) - 1)
     def _():
@@ -176,26 +215,29 @@
 
 
 def grad_call(kernel, ids, pair, others, other_specs, outs, out_specs, scratch):
-    heads, _, rows, width = pair.shape
-    sources = heads // 2 if heads % 2 == 0 else heads
-    return pl.pallas_call(
-        kernel,
+    heads = len(pair)
+    _, rows, width = pair[0].shape
+    scratch = scratch + [
+        pltpu.VMEM((heads, 2, rows, width), bf16),
+        pltpu.SemaphoreType.DMA((heads,)),
+    ]
+    return pl.pallas_call(
+        functools.partial(kernel, heads),
         grid_spec=pltpu.PrefetchScalarGridSpec(
             num_scalar_prefetch=1,
-            grid=(heads // sources,),
-            in_specs=[pl.BlockSpec((sources, 2, rows, width), lambda i, ids: (i, 0, 0, 0))]
-            + other_specs,
+            grid=(2,),
+            in_specs=[pl.BlockSpec(memory_space=pl.ANY)] * heads + other_specs,
             out_specs=out_specs,
             scratch_shapes=scratch,
         ),
         out_shape=outs,
         cost_estimate=cost(12 * heads * rows * width * width, 4 * heads * rows * width),
         compiler_params=pltpu.CompilerParams(vmem_limit_bytes=60 << 20),
-    )(ids, pair, *others)
+    )(ids, *pair, *others)
 
 
 def gradients_first(ids, pair, weights):
-    width = pair.shape[-1]
+    width = pair[0].shape[-1]
     weight = pl.BlockSpec((1, width, width), lambda i, ids: (ids[0], 0, 0))
     full = pl.BlockSpec((width, width), lambda i, ids: (0, 0))
     outs = [jax.ShapeDtypeStruct((width, width), f32)] * 3
@@ -204,7 +246,7 @@
 
 
 def gradients_last(ids, pair, carried):
-    width = pair.shape[-1]
+    width = pair[0].shape[-1]
     rows = width // 2
     full = pl.BlockSpec((width, width), lambda i, ids: (0, 0))
     half = pl.BlockSpec((rows, width), lambda i, ids: (0, 0))
@@ -256,10 +298,34 @@
     f_ref[...] = (pre1 * jax.nn.sigmoid(pre1) * pre3).astype(bf16)
 
 
-def output_kernel(f_ref, u2_ref, o_ref):
+def output_kernel(ids, f_ref, u2_ref, *o_refs):
     out = mm(f_ref[...], u2_ref[...])
     factor = lax.rsqrt(jnp.mean(out * out, axis=-1, keepdims=True) + epsilon)
-    o_ref[...] = (out * factor).astype(bf16)
+    for place, o_ref in enumerate(o_refs):
+
+        @pl.when(pl.program_id(0) == place)
+        def _():
+            o_ref[...] = (out * factor).astype(bf16)
+
+
+def outputs(ids, gated, weight, start, count, heads):
+    tokens, width = gated.shape
+    rows = tokens // heads
+    return pl.pallas_call(
+        output_kernel,
+        grid_spec=pltpu.PrefetchScalarGridSpec(
+            num_scalar_prefetch=1,
+            grid=(count,),
+            in_specs=[
+                pl.BlockSpec((rows, width), lambda i, ids: (ids[2] ^ (start + i), 0)),
+                pl.BlockSpec((width, width), lambda i, ids: (0, 0)),
+            ],
+            out_specs=[pl.BlockSpec((rows, width), lambda i, ids: (0, 0))] * count,
+        ),
+        out_shape=[jax.ShapeDtypeStruct((rows, width), bf16)] * count,
+        cost_estimate=cost(2 * count * rows * width * width, 4 * count * rows * width),
+        compiler_params=pltpu.CompilerParams(vmem_limit_bytes=60 << 20),
+    )(ids, gated, weight)
 
 
 def over_tokens(kernel, x, *weights):
@@ -321,12 +387,18 @@
     ids = jnp.stack([
         lax.axis_index("l1") * sizes["l2"] + lax.axis_index("l2"),
         (lax.axis_index(axis) >> bit) & 1,
+        lax.axis_index(("head", "l1", "l2")),
     ]).astype(jnp.int32)
+
+    def swap(block, k):
+        pairs = [(i, i ^ k) for i in range(heads)]
+        return lax.ppermute(block, ("head", "l1", "l2"), pairs)
+
     pairs = []
     block = keys.shape[0] // 4
     for start, count in ((0, 3), (3, 1)):
-        pair = prepared_pair(keys, values, rates, k_gain[None], start, count, block)
-        pairs.append(exchange(pair))
+        pair = prepared_pair(ids, keys, values, rates, k_gain[None], start, count, block)
+        pairs.append([pair[0]] + [swap(pair[k], k) for k in reversed(range(1, heads))])
     ready = prepared_queries(queries, q_gain[None], heads)
     query_local = exchange(ready)
     carried = gradients_first(ids, pairs[0], (w_first, w_second, w_third))
@@ -338,8 +410,12 @@
     new_third = updated(ids, full_third, w_third)
     gated = over_tokens(gate_kernel, query_local.reshape(-1, width), new_first, new_third)
     new_second = updated(ids, full_second, w_second)
-    normed = over_tokens(output_kernel, gated, new_second)
-    return back_to_columns(exchange(normed.reshape(heads, -1, width)))
+    far = heads // 2
+    blocks = outputs(ids, gated, new_second, far, heads - far, heads)
+    back = [swap(block, far + k) for k, block in enumerate(blocks)]
+    blocks = outputs(ids, gated, new_second, 0, far, heads)
+    near = [blocks[0]] + [swap(block, k) for k, block in enumerate(blocks) if k]
+    return back_to_columns(ids, near + back)
 
 
 def solution(mesh):

time: 263 us -> 282 us (1.072)
  blocking collectives: 36.6 us -> 0 us
  waiting for transfers between devices: 106 us -> 135 us
  starting transfers between devices: 29.7 us -> 46.5 us
  Pallas kernels: 82.9 us -> 91.6 us
    ppermute x0 -> x21, waiting for transfers between devices: none -> 85.3 us  [swap(): return lax.ppermute(block, ('head', 'l1', 'l2'), pairs)]
    all_to_all x2 -> x0, waiting for transfers between devices: 54.1 us -> none  [per_device(): pairs.append(exchange(pair))]
    all_to_all x1 -> x0, blocking collectives: 36.6 us -> none  [per_device(): return back_to_columns(exchange(normed.reshape(heads, -1, width)))]
    ppermute x0 -> x21, starting transfers between devices: none -> 25.5 us  [swap(): return lax.ppermute(block, ('head', 'l1', 'l2'), pairs)]
    pallas_call x5 -> x7, Pallas kernels: 38.9 us -> 53.6 us  [the longest x2 27.1 us: grad_call(): pl.pallas_call(functools.partial(kernel, heads), grid_spec=pltpu.Prefetch...]
    all_to_all x2 -> x0, starting transfers between devices: 9.79 us -> none  [per_device(): pairs.append(exchange(pair))]
    pallas_call x2 -> x1, Pallas kernels: 14 us -> 7.81 us  [over_tokens(): pl.pallas_call(kernel, grid=(tokens // block,), in_specs=[tile] + [full]...]
  transfers between devices with their start and end apart: 12 -> 31, of which waited for: 8 -> 16; matrix products, arithmetic and copies ran while one was open for 1% -> 1% of each run, Pallas kernels for 23% -> 24%
where the time goes in v3:
time: 282 us; the launch traced here: 281 us
  waiting for transfers between devices  135 us (48%)
  Pallas kernels  91.6 us (32%)
  starting transfers between devices  46.5 us (16%)
  local copies, waits for them, and re-layouts  3.68 us (1%)
  other arithmetic  3.57 us (1%)
    ppermute x21, waiting for transfers between devices, swap(): return lax.ppermute(block, ('head', 'l1', 'l2'), pairs)  85.3 us
    ppermute x6, waiting for transfers between devices, summed(): came = lax.ppermute(send, axis, pairs)  49.8 us
    pallas_call x2, Pallas kernels, grad_call(): pl.pallas_call(functools.partial(kernel, heads), grid_spec=pltpu.Prefetch...  27.1 us
    pallas_call x3, Pallas kernels, updated(): pl.pallas_call(newton_kernel, grid_spec=pltpu.PrefetchScalarGridSpec(num_...  25.7 us
    ppermute x21, starting transfers between devices, swap(): return lax.ppermute(block, ('head', 'l1', 'l2'), pairs)  25.5 us
    ppermute x6, starting transfers between devices, summed(): came = lax.ppermute(send, axis, pairs)  12.6 us
    pallas_call x2, Pallas kernels, outputs(): pl.pallas_call(output_kernel, grid_spec=pltpu.PrefetchScalarGridSpec(num_...  11.6 us
    pallas_call x2, Pallas kernels, prepared_pair(): pl.pallas_call(pair_kernel, grid_spec=pltpu.PrefetchScalarGridSpec(num_sc...  10.1 us
  transfers between devices with their start and end apart: 31, of which 16 were waited for; matrix products, arithmetic and copies ran while one was open for 1% of the time, Pallas kernels for 24%

profile of v3, /device:TPU:0, one launch (start us, length us, event | category | flops | bytes accessed | tf_op | source)
XLA Modules:
  0.0 280.8 jit_solution(622216848955453320)
XLA Ops:
  2.0 6.5 %shard_map.93 = (bf16[2,192,640]{2,1,0:T(8,128)(2,1)}, bf16[2,192,640]{2,1,0:T(8,128)(2,1)}, bf16[2,192,640]{2,1,0:T(8,128)(2,1)}, bf16[2,192,640]{2,1,0:T(8,128...) custom-call(s32[3]{0:T(128)} %pad_add_fusion.ids, ...), custom_call_target="tpu_custom_call" | custom-call | flops 11796480 | bytes 7864320 | tf_op jit(solution)/shard_map/pallas_call | solution.py:85
  8.5 3.0 %collective-permute-start.10 = (bf16[2,192,640]{2,1,0:T(8,128)(2,1)}, bf16[2,192,640]{2,1,0:T(8,128)(2,1)S(1)}, u32[]{:S(2)}, u32[]{:S(2)}) collective-permute-start(bf16[2,192,640]{2,1,0:T(8,128)(2,1)} %get-tuple-element.53), channel_id=1, source_target_pairs={{0,16},{1,17},{4,20},{5,21},{16,0},{17,1},{20,4},{21,5},{2,18},{3,... | collective-permute-start | bytes 1474568 | tf_op jit(solution)/shard_map/ppermute | solution.py:395
  12.2 4.5 %shard_map.91 = bf16[8,256,640]{2,1,0:T(8,128)(2,1)} custom-call(bf16[256,5120]{1,0:T(8,128)(2,1)} %x_ref.1, f32[1,5120]{1,0:T(1,128)} %bitcast.9), custom_call_target="tpu_custom_call" | custom-call | flops 10485760 | bytes 5242880 | tf_op jit(solution)/shard_map/pallas_call | solution.py:66
  16.8 3.6 %all-to-all-start = ((bf16[8,256,640]{2,1,0:T(8,128)(2,1)}), bf16[8,256,640]{2,1,0:T(8,128)(2,1)S(1)}, u32[]{:S(2)}, u32[]{:S(2)}) async-start(bf16[8,256,640]{2,1,0:T(8,128)(2,1)} %shard_map.91), calls=%async_computation | async-start | bytes 5242880 | tf_op jit(solution)/shard_map/all_to_all | solution.py:403
  20.4 3.6 %shard_map.92 = (bf16[2,64,640]{2,1,0:T(8,128)(2,1)}, bf16[2,64,640]{2,1,0:T(8,128)(2,1)}, bf16[2,64,640]{2,1,0:T(8,128)(2,1)}, bf16[2,64,640]{2,1,0:T(8,128)(2,...) custom-call(s32[3]{0:T(128)} %pad_add_fusion.ids, ...), custom_call_target="tpu_custom_call" | custom-call | flops 3932160 | bytes 2621440 | tf_op jit(solution)/shard_map/pallas_call | solution.py:85
  28.6 27.5 %collective-permute-done.refs_1_ = bf16[2,64,640]{2,1,0:T(8,128)(2,1)S(1)} collective-permute-done((bf16[2,64,640]{2,1,0:T(8,128)(2,1)}, bf16[2,64,640]{2,1,0:T(8,128)(2,1)S(1)}, u32[]{:S(2)}, u32[]{:S(2)}) %collective-permute-start) | collective-permute-done | bytes 163872 | tf_op jit(solution)/shard_map/ppermute | solution.py:395
  56.5 3.7 %collective-permute-done.1.refs_2_ = bf16[2,64,640]{2,1,0:T(8,128)(2,1)S(1)} collective-permute-done((bf16[2,64,640]{2,1,0:T(8,128)(2,1)}, bf16[2,64,640]{2,1,0:T(8,128)(2,1)S(1)}, u32[]{:S(2)}, u32[]{:S(2)}) %collective-permute-start.1) | collective-permute-done | bytes 163872 | tf_op jit(solution)/shard_map/ppermute | solution.py:395
  64.3 6.7 %collective-permute-done.12.refs_6_ = bf16[2,192,640]{2,1,0:T(8,128)(2,1)S(1)} collective-permute-done((bf16[2,192,640]{2,1,0:T(8,128)(2,1)}, bf16[2,192,640]{2,1,0:T(8,128)(2,1)S(1)}, u32[]{:S(2)}, u32[]{:S(2)}) %collective-permute-start.12) | collective-permute-done | bytes 491552 | tf_op jit(solution)/shard_map/ppermute | solution.py:395
  72.6 8.2 %collective-permute-done.7.refs_1_ = bf16[2,192,640]{2,1,0:T(8,128)(2,1)} collective-permute-done((bf16[2,192,640]{2,1,0:T(8,128)(2,1)}, bf16[2,192,640]{2,1,0:T(8,128)(2,1)}, u32[]{:S(2)}, u32[]{:S(2)}) %collective-permute-start.7) | collective-permute-done | bytes 491552 | tf_op jit(solution)/shard_map/ppermute | solution.py:395
  82.4 9.6 %collective-permute-done.8.refs_2_ = bf16[2,192,640]{2,1,0:T(8,128)(2,1)} collective-permute-done((bf16[2,192,640]{2,1,0:T(8,128)(2,1)}, bf16[2,192,640]{2,1,0:T(8,128)(2,1)}, u32[]{:S(2)}, u32[]{:S(2)}) %collective-permute-start.8) | collective-permute-done | bytes 491552 | tf_op jit(solution)/shard_map/ppermute | solution.py:395
  93.2 4.1 %collective-permute-done.9.refs_3_ = bf16[2,192,640]{2,1,0:T(8,128)(2,1)} collective-permute-done((bf16[2,192,640]{2,1,0:T(8,128)(2,1)}, bf16[2,192,640]{2,1,0:T(8,128)(2,1)}, u32[]{:S(2)}, u32[]{:S(2)}) %collective-permute-start.9) | collective-permute-done | bytes 491552 | tf_op jit(solution)/shard_map/ppermute | solution.py:395
  98.2 17.1 %shard_map.94 = (f32[640,640]{1,0:T(8,128)}, f32[640,640]{1,0:T(8,128)}, f32[640,640]{1,0:T(8,128)}, bf16[640,640]{1,0:T(8,128)(2,1)}, bf16[640,640]{1,0:T(8,128)(2,1)}, /*index=5*/bf16[640,640]{1,0:T(8,128)(2,1)}) custom-call(s32[3]{0:T(128)} %pad_add_fusion.ids, bf16[2,192,640]{2,1,0:T(8,128)(2,1)} %get-tuple-element.49.refs_0_, ...), custom_call_target="tpu_custom_call" | custom-call | flops 7549747200 | bytes 3932160 | tf_op jit(solution)/shard_map/pallas_call | solution.py:224
  115.3 10.0 %shard_map.95 = (bf16[320,640]{1,0:T(8,128)(2,1)}, f32[320,640]{1,0:T(8,128)}, bf16[320,640]{1,0:T(8,128)(2,1)}, f32[320,640]{1,0:T(8,128)}, bf16[320,640]{1,0:T(8,128)(2,1)}, /*index=5*/f32[320,640]{1,0:T(8,128)}) custom-call(s32[3]{0:T(128)} %pad_add_fusion.ids, bf16[2,64,640]{2,1,0:T(8,128)(2,1)} %get-tuple-element.41.refs_0_, ...), custom_call_target="tpu_custom_call" | custom-call | flops 2516582400 | bytes 1310720 | tf_op jit(solution)/shard_map/pallas_call | solution.py:224
  129.3 8.7 %collective-permute-done.20 = bf16[320,640]{1,0:T(8,128)(2,1)S(1)} collective-permute-done((bf16[320,640]{1,0:T(8,128)(2,1)}, bf16[320,640]{1,0:T(8,128)(2,1)S(1)}, u32[]{:S(2)}, u32[]{:S(2)}) %collective-permute-start.20) | collective-permute-done | bytes 409632 | tf_op jit(solution)/shard_map/ppermute | solution.py:350
  139.3 2.9 %collective-permute-start.21 = (bf16[320,640]{1,0:T(8,128)(2,1)S(1)}, bf16[320,640]{1,0:T(8,128)(2,1)S(1)}, u32[]{:S(2)}, u32[]{:S(2)}) collective-permute-start(bf16[320,640]{1,0:T(8,128)(2,1)S(1)} %fusion.2), channel_id=1, source_target_pairs={{0,8},{8,0},{1,9},{9,1},{2,10},{10,2},{3,11},{11,3},{4,12},{12,4},... | collective-permute-start | bytes 1228808 | tf_op jit(solution)/shard_map/ppermute | solution.py:350
  142.2 4.6 %collective-permute-done.17 = bf16[320,640]{1,0:T(8,128)(2,1)S(1)} collective-permute-done((bf16[320,640]{1,0:T(8,128)(2,1)}, bf16[320,640]{1,0:T(8,128)(2,1)S(1)}, u32[]{:S(2)}, u32[]{:S(2)}) %collective-permute-start.17) | collective-permute-done | bytes 409632 | tf_op jit(solution)/shard_map/ppermute | solution.py:350
  148.1 2.9 %collective-permute-start.18 = (bf16[320,640]{1,0:T(8,128)(2,1)S(1)}, bf16[320,640]{1,0:T(8,128)(2,1)S(1)}, u32[]{:S(2)}, u32[]{:S(2)}) collective-permute-start(bf16[320,640]{1,0:T(8,128)(2,1)S(1)} %fusion.1), channel_id=1, source_target_pairs={{0,8},{8,0},{1,9},{9,1},{2,10},{10,2},{3,11},{11,3},{4,12},{12,4},... | collective-permute-start | bytes 1228808 | tf_op jit(solution)/shard_map/ppermute | solution.py:350
  151.0 3.7 %collective-permute-done.14 = bf16[320,640]{1,0:T(8,128)(2,1)S(1)} collective-permute-done((bf16[320,640]{1,0:T(8,128)(2,1)}, bf16[320,640]{1,0:T(8,128)(2,1)S(1)}, u32[]{:S(2)}, u32[]{:S(2)}) %collective-permute-start.14) | collective-permute-done | bytes 409632 | tf_op jit(solution)/shard_map/ppermute | solution.py:350
  154.8 2.9 %collective-permute-start.15 = (bf16[320,640]{1,0:T(8,128)(2,1)S(1)}, bf16[320,640]{1,0:T(8,128)(2,1)S(1)}, u32[]{:S(2)}, u32[]{:S(2)}) collective-permute-start(bf16[320,640]{1,0:T(8,128)(2,1)S(1)} %fusion), channel_id=1, source_target_pairs={{0,8},{8,0},{1,9},{9,1},{2,10},{10,2},{3,11},{11,3},{4,12},{12,4},... | collective-permute-start | bytes 1228808 | tf_op jit(solution)/shard_map/ppermute | solution.py:350
  157.7 19.8 %collective-permute-done.21 = bf16[320,640]{1,0:T(8,128)(2,1)S(1)} collective-permute-done((bf16[320,640]{1,0:T(8,128)(2,1)S(1)}, bf16[320,640]{1,0:T(8,128)(2,1)S(1)}, u32[]{:S(2)}, u32[]{:S(2)}) %collective-permute-start.21) | collective-permute-done | bytes 409632 | tf_op jit(solution)/shard_map/ppermute | solution.py:350
  179.2 7.1 %collective-permute-done.18 = bf16[320,640]{1,0:T(8,128)(2,1)S(1)} collective-permute-done((bf16[320,640]{1,0:T(8,128)(2,1)S(1)}, bf16[320,640]{1,0:T(8,128)(2,1)S(1)}, u32[]{:S(2)}, u32[]{:S(2)}) %collective-permute-start.18) | collective-permute-done | bytes 409632 | tf_op jit(solution)/shard_map/ppermute | solution.py:350
  187.9 6.0 %collective-permute-done.15 = bf16[320,640]{1,0:T(8,128)(2,1)S(1)} collective-permute-done((bf16[320,640]{1,0:T(8,128)(2,1)S(1)}, bf16[320,640]{1,0:T(8,128)(2,1)S(1)}, u32[]{:S(2)}, u32[]{:S(2)}) %collective-permute-start.15) | collective-permute-done | bytes 409632 | tf_op jit(solution)/shard_map/ppermute | solution.py:350
  195.7 8.5 %shard_map.99.u2_ref = bf16[640,640]{1,0:T(8,128)(2,1)} custom-call(s32[3]{0:T(128)} %pad_add_fusion.ids, bf16[320,640]{1,0:T(8,128)(2,1)} %copy-done.4, bf16[320,640]{1,0:T(8,128)(2,1)} %collective-permute-done.22.other_ref, f32[4,640,640]{2,1,0:T(8,128)} %w_ref.5), custom_call_target="tpu_custom_call" | custom-call | flops 3145728000 | bytes 3276800 | tf_op jit(solution)/shard_map/pallas_call | solution.py:280
  204.2 8.5 %shard_map.97.u3_ref = bf16[640,640]{1,0:T(8,128)(2,1)} custom-call(s32[3]{0:T(128)} %pad_add_fusion.ids, bf16[320,640]{1,0:T(8,128)(2,1)} %copy-done.5, bf16[320,640]{1,0:T(8,128)(2,1)} %collective-permute-done.19.other_ref, f32[4,640,640]{2,1,0:T(8,128)} %w_ref.4), custom_call_target="tpu_custom_call" | custom-call | flops 3145728000 | bytes 3276800 | tf_op jit(solution)/shard_map/pallas_call | solution.py:280
  212.7 8.7 %shard_map.96.u1_ref = bf16[640,640]{1,0:T(8,128)(2,1)} custom-call(s32[3]{0:T(128)} %pad_add_fusion.ids, bf16[320,640]{1,0:T(8,128)(2,1)} %copy-done.6, bf16[320,640]{1,0:T(8,128)(2,1)} %collective-permute-done.16.other_ref, f32[4,640,640]{2,1,0:T(8,128)} %w_ref.3), custom_call_target="tpu_custom_call" | custom-call | flops 3145728000 | bytes 3276800 | tf_op jit(solution)/shard_map/pallas_call | solution.py:280
  222.9 7.8 %shard_map.98.f_ref = bf16[2048,640]{1,0:T(8,128)(2,1)} custom-call(bf16[2048,640]{1,0:T(8,128)(2,1)} %bitcast.6, bf16[640,640]{1,0:T(8,128)(2,1)} %shard_map.96.u1_ref, bf16[640,640]{1,0:T(8,128)(2,1)} %shard_map.97.u3_ref), custom_call_target="tpu_custom_call" | custom-call | flops 3355443200 | bytes 5242880 | tf_op jit(solution)/shard_map/pallas_call | solution.py:336
  230.7 5.9 %shard_map.101 = (bf16[256,640]{1,0:T(8,128)(2,1)}, bf16[256,640]{1,0:T(8,128)(2,1)}, bf16[256,640]{1,0:T(8,128)(2,1)}, bf16[256,640]{1,0:T(8,128)(2,1)}) custom-call(s32[3]{0:T(128)} %pad_add_fusion.ids, bf16[2048,640]{1,0:T(8,128)(2,1)} %shard_map.98.f_ref, bf16[640,640]{1,0:T(8,128)(2,1)} %shard_map.99.u2_ref), custom_call_target="tpu_custom_call" | custom-call | flops 838860800 | bytes 2621440 | tf_op jit(solution)/shard_map/pallas_call | solution.py:314
  241.0 5.8 %shard_map.100 = (bf16[256,640]{1,0:T(8,128)(2,1)}, bf16[256,640]{1,0:T(8,128)(2,1)}, bf16[256,640]{1,0:T(8,128)(2,1)}, bf16[256,640]{1,0:T(8,128)(2,1)}) custom-call(s32[3]{0:T(128)} %pad_add_fusion.ids, bf16[2048,640]{1,0:T(8,128)(2,1)} %shard_map.98.f_ref, bf16[640,640]{1,0:T(8,128)(2,1)} %shard_map.99.u2_ref), custom_call_target="tpu_custom_call" | custom-call | flops 838860800 | bytes 2621440 | tf_op jit(solution)/shard_map/pallas_call | solution.py:314
  246.9 14.5 %collective-permute-done.26.refs_4_ = bf16[256,640]{1,0:T(8,128)(2,1)S(1)} collective-permute-done((bf16[256,640]{1,0:T(8,128)(2,1)}, bf16[256,640]{1,0:T(8,128)(2,1)S(1)}, u32[]{:S(2)}, u32[]{:S(2)}) %collective-permute-start.26) | collective-permute-done | bytes 327712 | tf_op jit(solution)/shard_map/ppermute | solution.py:395
  262.1 3.4 %collective-permute-done.27.refs_5_ = bf16[256,640]{1,0:T(8,128)(2,1)S(1)} collective-permute-done((bf16[256,640]{1,0:T(8,128)(2,1)}, bf16[256,640]{1,0:T(8,128)(2,1)S(1)}, u32[]{:S(2)}, u32[]{:S(2)}) %collective-permute-start.27) | collective-permute-done | bytes 327712 | tf_op jit(solution)/shard_map/ppermute | solution.py:395
  268.7 6.6 %collective-permute-done.25.refs_3_ = bf16[256,640]{1,0:T(8,128)(2,1)S(1)} collective-permute-done((bf16[256,640]{1,0:T(8,128)(2,1)}, bf16[256,640]{1,0:T(8,128)(2,1)S(1)}, u32[]{:S(2)}, u32[]{:S(2)}) %collective-permute-start.25) | collective-permute-done | bytes 327712 | tf_op jit(solution)/shard_map/ppermute | solution.py:395
  276.0 4.7 %shard_map.102 = bf16[256,5120]{1,0:T(8,128)(2,1)} custom-call(s32[3]{0:T(128)} %pad_add_fusion.ids, bf16[256,640]{1,0:T(8,128)(2,1)} %get-tuple-element.69.refs_0_, bf16[256,640]{1,0:T(8,128)(2,1)} %copy-done.11, bf16[256,640]{1,0:T(8,128)(2,1)} %copy-done.12, bf16[256,640]{1,0:T(8,128)(2,1)} %copy-done.13, bf16[256,640]{1,0:T(8,128)(2,1)} %copy-done.7, ...), custom_call_target="tpu_custom_call" | custom-call | flops 1310720 | bytes 5242880 | tf_op jit(solution)/shard_map/pallas_call | solution.py:114
  (86 shorter events, 39.5 us)
Async XLA Ops:
  8.5 53.9 %collective-permute-start.10 = (bf16[2,192,640]{2,1,0:T(8,128)(2,1)}, bf16[2,192,640]{2,1,0:T(8,128)(2,1)S(1)}, u32[]{:S(2)}, u32[]{:S(2)}) collective-permute-start(bf16[2,192,640]{2,1,0:T(8,128)(2,1)} %get-tuple-element.53), channel_id=1, source_target_pairs={{0,16},{1,17},{4,20},{5,21},{16,0},{17,1},{20,4},{21,5},{2,18},{3,... | collective-permute-start | bytes 1474568 | tf_op jit(solution)/shard_map/ppermute | solution.py:395
  11.5 51.0 %collective-permute-start.11 = (bf16[2,192,640]{2,1,0:T(8,128)(2,1)}, bf16[2,192,640]{2,1,0:T(8,128)(2,1)}, u32[]{:S(2)}, u32[]{:S(2)}) collective-permute-start(bf16[2,192,640]{2,1,0:T(8,128)(2,1)} %get-tuple-element.54), channel_id=1, source_target_pairs={{0,5},{1,4},{4,1},{5,0},{16,21},{17,20},{20,17},{21,16},{2,7},{3,6... | collective-permute-start | bytes 1474568 | tf_op jit(solution)/shard_map/ppermute | solution.py:395
  16.8 204.6 %all-to-all-start = ((bf16[8,256,640]{2,1,0:T(8,128)(2,1)}), bf16[8,256,640]{2,1,0:T(8,128)(2,1)S(1)}, u32[]{:S(2)}, u32[]{:S(2)}) async-start(bf16[8,256,640]{2,1,0:T(8,128)(2,1)} %shard_map.91), calls=%async_computation | async-start | bytes 5242880 | tf_op jit(solution)/shard_map/all_to_all | solution.py:403
  24.0 32.1 %collective-permute-start = (bf16[2,64,640]{2,1,0:T(8,128)(2,1)}, bf16[2,64,640]{2,1,0:T(8,128)(2,1)S(1)}, u32[]{:S(2)}, u32[]{:S(2)}) collective-permute-start(bf16[2,64,640]{2,1,0:T(8,128)(2,1)} %get-tuple-element.42), channel_id=1, source_target_pairs={{0,21},{1,20},{4,17},{5,16},{16,5},{17,4},{20,1},{21,0},{2,23},{3,... | collective-permute-start | bytes 491528 | tf_op jit(solution)/shard_map/ppermute | solution.py:395
  26.6 33.6 %collective-permute-start.1 = (bf16[2,64,640]{2,1,0:T(8,128)(2,1)}, bf16[2,64,640]{2,1,0:T(8,128)(2,1)S(1)}, u32[]{:S(2)}, u32[]{:S(2)}) collective-permute-start(bf16[2,64,640]{2,1,0:T(8,128)(2,1)} %get-tuple-element.43), channel_id=1, source_target_pairs={{0,20},{1,21},{4,16},{5,17},{16,4},{17,5},{20,0},{21,1},{2,22},{3,... | collective-permute-start | bytes 491528 | tf_op jit(solution)/shard_map/ppermute | solution.py:395
  27.4 43.6 %collective-permute-start.12 = (bf16[2,192,640]{2,1,0:T(8,128)(2,1)}, bf16[2,192,640]{2,1,0:T(8,128)(2,1)S(1)}, u32[]{:S(2)}, u32[]{:S(2)}) collective-permute-start(bf16[2,192,640]{2,1,0:T(8,128)(2,1)} %get-tuple-element.55), channel_id=1, source_target_pairs={{0,4},{1,5},{4,0},{5,1},{16,20},{17,21},{20,16},{21,17},{2,6},{3,7... | collective-permute-start | bytes 1474568 | tf_op jit(solution)/shard_map/ppermute | solution.py:395
  56.1 59.2 %copy-start.16 = (bf16[2,64,640]{2,1,0:T(8,128)(2,1)}, bf16[2,64,640]{2,1,0:T(8,128)(2,1)S(1)}, u32[]{:S(2)}) copy-start(bf16[2,64,640]{2,1,0:T(8,128)(2,1)S(1)} %collective-permute-done.refs_1_) | copy-start | bytes 491524
  56.1 15.0 %collective-permute-start.13 = (bf16[2,192,640]{2,1,0:T(8,128)(2,1)}, bf16[2,192,640]{2,1,0:T(8,128)(2,1)}, u32[]{:S(2)}, u32[]{:S(2)}) collective-permute-start(bf16[2,192,640]{2,1,0:T(8,128)(2,1)} %get-tuple-element.56), channel_id=1, source_target_pairs={{0,1},{1,0},{4,5},{5,4},{16,17},{17,16},{20,21},{21,20},{2,3},{3,2... | collective-permute-start | bytes 1474568 | tf_op jit(solution)/shard_map/ppermute | solution.py:395
  60.2 20.7 %collective-permute-start.7 = (bf16[2,192,640]{2,1,0:T(8,128)(2,1)}, bf16[2,192,640]{2,1,0:T(8,128)(2,1)}, u32[]{:S(2)}, u32[]{:S(2)}) collective-permute-start(bf16[2,192,640]{2,1,0:T(8,128)(2,1)} %get-tuple-element.50), channel_id=1, source_target_pairs={{0,21},{1,20},{4,17},{5,16},{16,5},{17,4},{20,1},{21,0},{2,23},{3,... | collective-permute-start | bytes 1474568 | tf_op jit(solution)/shard_map/ppermute | solution.py:395
  62.3 29.6 %collective-permute-start.8 = (bf16[2,192,640]{2,1,0:T(8,128)(2,1)}, bf16[2,192,640]{2,1,0:T(8,128)(2,1)}, u32[]{:S(2)}, u32[]{:S(2)}) collective-permute-start(bf16[2,192,640]{2,1,0:T(8,128)(2,1)} %get-tuple-element.51), channel_id=1, source_target_pairs={{0,20},{1,21},{4,16},{5,17},{16,4},{17,5},{20,0},{21,1},{2,22},{3,... | collective-permute-start | bytes 1474568 | tf_op jit(solution)/shard_map/ppermute | solution.py:395
  62.5 34.9 %collective-permute-start.9 = (bf16[2,192,640]{2,1,0:T(8,128)(2,1)}, bf16[2,192,640]{2,1,0:T(8,128)(2,1)}, u32[]{:S(2)}, u32[]{:S(2)}) collective-permute-start(bf16[2,192,640]{2,1,0:T(8,128)(2,1)} %get-tuple-element.52), channel_id=1, source_target_pairs={{0,17},{1,16},{4,21},{5,20},{16,1},{17,0},{20,5},{21,4},{2,19},{3,... | collective-permute-start | bytes 1474568 | tf_op jit(solution)/shard_map/ppermute | solution.py:395
  71.0 44.3 %collective-permute-start.2 = (bf16[2,64,640]{2,1,0:T(8,128)(2,1)}, bf16[2,64,640]{2,1,0:T(8,128)(2,1)}, u32[]{:S(2)}, u32[]{:S(2)}) collective-permute-start(bf16[2,64,640]{2,1,0:T(8,128)(2,1)} %get-tuple-element.44), channel_id=1, source_target_pairs={{0,17},{1,16},{4,21},{5,20},{16,1},{17,0},{20,5},{21,4},{2,19},{3,... | collective-permute-start | bytes 491528 | tf_op jit(solution)/shard_map/ppermute | solution.py:395
  71.0 44.3 %collective-permute-start.3 = (bf16[2,64,640]{2,1,0:T(8,128)(2,1)}, bf16[2,64,640]{2,1,0:T(8,128)(2,1)}, u32[]{:S(2)}, u32[]{:S(2)}) collective-permute-start(bf16[2,64,640]{2,1,0:T(8,128)(2,1)} %get-tuple-element.45), channel_id=1, source_target_pairs={{0,16},{1,17},{4,20},{5,21},{16,0},{17,1},{20,4},{21,5},{2,18},{3,... | collective-permute-start | bytes 491528 | tf_op jit(solution)/shard_map/ppermute | solution.py:395
  80.9 34.5 %collective-permute-start.4 = (bf16[2,64,640]{2,1,0:T(8,128)(2,1)}, bf16[2,64,640]{2,1,0:T(8,128)(2,1)}, u32[]{:S(2)}, u32[]{:S(2)}) collective-permute-start(bf16[2,64,640]{2,1,0:T(8,128)(2,1)} %get-tuple-element.46), channel_id=1, source_target_pairs={{0,5},{1,4},{4,1},{5,0},{16,21},{17,20},{20,17},{21,16},{2,7},{3,6... | collective-permute-start | bytes 491528 | tf_op jit(solution)/shard_map/ppermute | solution.py:395
  91.9 23.4 %collective-permute-start.5 = (bf16[2,64,640]{2,1,0:T(8,128)(2,1)}, bf16[2,64,640]{2,1,0:T(8,128)(2,1)}, u32[]{:S(2)}, u32[]{:S(2)}) collective-permute-start(bf16[2,64,640]{2,1,0:T(8,128)(2,1)} %get-tuple-element.47), channel_id=1, source_target_pairs={{0,4},{1,5},{4,0},{5,1},{16,20},{17,21},{20,16},{21,17},{2,6},{3,7... | collective-permute-start | bytes 491528 | tf_op jit(solution)/shard_map/ppermute | solution.py:395
  97.3 18.0 %collective-permute-start.6 = (bf16[2,64,640]{2,1,0:T(8,128)(2,1)}, bf16[2,64,640]{2,1,0:T(8,128)(2,1)}, u32[]{:S(2)}, u32[]{:S(2)}) collective-permute-start(bf16[2,64,640]{2,1,0:T(8,128)(2,1)} %get-tuple-element.48), channel_id=1, source_target_pairs={{0,1},{1,0},{4,5},{5,4},{16,17},{17,16},{20,21},{21,20},{2,3},{3,2... | collective-permute-start | bytes 491528 | tf_op jit(solution)/shard_map/ppermute | solution.py:395
  125.4 12.6 %collective-permute-start.20 = (bf16[320,640]{1,0:T(8,128)(2,1)}, bf16[320,640]{1,0:T(8,128)(2,1)S(1)}, u32[]{:S(2)}, u32[]{:S(2)}) collective-permute-start(bf16[320,640]{1,0:T(8,128)(2,1)} %get-tuple-element.68), channel_id=1, source_target_pairs={{0,2},{2,0},{1,3},{3,1},{4,6},{6,4},{5,7},{7,5},{8,10},{10,8},{9,1... | collective-permute-start | bytes 1228808 | tf_op jit(solution)/shard_map/ppermute | solution.py:350
  127.3 19.5 %collective-permute-start.17 = (bf16[320,640]{1,0:T(8,128)(2,1)}, bf16[320,640]{1,0:T(8,128)(2,1)S(1)}, u32[]{:S(2)}, u32[]{:S(2)}) collective-permute-start(bf16[320,640]{1,0:T(8,128)(2,1)} %get-tuple-element.66), channel_id=1, source_target_pairs={{0,2},{2,0},{1,3},{3,1},{4,6},{6,4},{5,7},{7,5},{8,10},{10,8},{9,1... | collective-permute-start | bytes 1228808 | tf_op jit(solution)/shard_map/ppermute | solution.py:350
  127.5 27.2 %collective-permute-start.14 = (bf16[320,640]{1,0:T(8,128)(2,1)}, bf16[320,640]{1,0:T(8,128)(2,1)S(1)}, u32[]{:S(2)}, u32[]{:S(2)}) collective-permute-start(bf16[320,640]{1,0:T(8,128)(2,1)} %get-tuple-element.64), channel_id=1, source_target_pairs={{0,2},{2,0},{1,3},{3,1},{4,6},{6,4},{5,7},{7,5},{8,10},{10,8},{9,1... | collective-permute-start | bytes 1228808 | tf_op jit(solution)/shard_map/ppermute | solution.py:350
  139.3 38.2 %collective-permute-start.21 = (bf16[320,640]{1,0:T(8,128)(2,1)S(1)}, bf16[320,640]{1,0:T(8,128)(2,1)S(1)}, u32[]{:S(2)}, u32[]{:S(2)}) collective-permute-start(bf16[320,640]{1,0:T(8,128)(2,1)S(1)} %fusion.2), channel_id=1, source_target_pairs={{0,8},{8,0},{1,9},{9,1},{2,10},{10,2},{3,11},{11,3},{4,12},{12,4},... | collective-permute-start | bytes 1228808 | tf_op jit(solution)/shard_map/ppermute | solution.py:350
  148.1 38.1 %collective-permute-start.18 = (bf16[320,640]{1,0:T(8,128)(2,1)S(1)}, bf16[320,640]{1,0:T(8,128)(2,1)S(1)}, u32[]{:S(2)}, u32[]{:S(2)}) collective-permute-start(bf16[320,640]{1,0:T(8,128)(2,1)S(1)} %fusion.1), channel_id=1, source_target_pairs={{0,8},{8,0},{1,9},{9,1},{2,10},{10,2},{3,11},{11,3},{4,12},{12,4},... | collective-permute-start | bytes 1228808 | tf_op jit(solution)/shard_map/ppermute | solution.py:350
  154.8 39.1 %collective-permute-start.15 = (bf16[320,640]{1,0:T(8,128)(2,1)S(1)}, bf16[320,640]{1,0:T(8,128)(2,1)S(1)}, u32[]{:S(2)}, u32[]{:S(2)}) collective-permute-start(bf16[320,640]{1,0:T(8,128)(2,1)S(1)} %fusion), channel_id=1, source_target_pairs={{0,8},{8,0},{1,9},{9,1},{2,10},{10,2},{3,11},{11,3},{4,12},{12,4},... | collective-permute-start | bytes 1228808 | tf_op jit(solution)/shard_map/ppermute | solution.py:350
  177.6 18.1 %collective-permute-start.22 = (bf16[320,640]{1,0:T(8,128)(2,1)S(1)}, bf16[320,640]{1,0:T(8,128)(2,1)}, u32[]{:S(2)}, u32[]{:S(2)}) collective-permute-start(bf16[320,640]{1,0:T(8,128)(2,1)S(1)} %add_convert_fusion.own_ref), channel_id=1, source_target_pairs={{0,2},{2,0},{1,3},{3,1},{4,6},{6,4},{5,7},{7,5},{8,10},{10,8},{9,1... | collective-permute-start | bytes 1228808 | tf_op jit(solution)/shard_map/ppermute | solution.py:364
  186.3 17.9 %collective-permute-start.19 = (bf16[320,640]{1,0:T(8,128)(2,1)S(1)}, bf16[320,640]{1,0:T(8,128)(2,1)}, u32[]{:S(2)}, u32[]{:S(2)}) collective-permute-start(bf16[320,640]{1,0:T(8,128)(2,1)S(1)} %add_convert_fusion.1.own_ref), channel_id=1, source_target_pairs={{0,2},{2,0},{1,3},{3,1},{4,6},{6,4},{5,7},{7,5},{8,10},{10,8},{9,1... | collective-permute-start | bytes 1228808 | tf_op jit(solution)/shard_map/ppermute | solution.py:364
  194.1 18.6 %collective-permute-start.16 = (bf16[320,640]{1,0:T(8,128)(2,1)S(1)}, bf16[320,640]{1,0:T(8,128)(2,1)}, u32[]{:S(2)}, u32[]{:S(2)}) collective-permute-start(bf16[320,640]{1,0:T(8,128)(2,1)S(1)} %add_convert_fusion.2.own_ref), channel_id=1, source_target_pairs={{0,2},{2,0},{1,3},{3,1},{4,6},{6,4},{5,7},{7,5},{8,10},{10,8},{9,1... | collective-permute-start | bytes 1228808 | tf_op jit(solution)/shard_map/ppermute | solution.py:364
  236.6 24.8 %collective-permute-start.26 = (bf16[256,640]{1,0:T(8,128)(2,1)}, bf16[256,640]{1,0:T(8,128)(2,1)S(1)}, u32[]{:S(2)}, u32[]{:S(2)}) collective-permute-start(bf16[256,640]{1,0:T(8,128)(2,1)} %get-tuple-element.73), channel_id=1, source_target_pairs={{0,16},{1,17},{4,20},{5,21},{16,0},{17,1},{20,4},{21,5},{2,18},{3,... | collective-permute-start | bytes 983048 | tf_op jit(solution)/shard_map/ppermute | solution.py:395
  238.1 27.4 %collective-permute-start.27 = (bf16[256,640]{1,0:T(8,128)(2,1)}, bf16[256,640]{1,0:T(8,128)(2,1)S(1)}, u32[]{:S(2)}, u32[]{:S(2)}) collective-permute-start(bf16[256,640]{1,0:T(8,128)(2,1)} %get-tuple-element.74), channel_id=1, source_target_pairs={{0,17},{1,16},{4,21},{5,20},{16,1},{17,0},{20,5},{21,4},{2,19},{3,... | collective-permute-start | bytes 983048 | tf_op jit(solution)/shard_map/ppermute | solution.py:395
  238.1 29.5 %collective-permute-start.28 = (bf16[256,640]{1,0:T(8,128)(2,1)}, bf16[256,640]{1,0:T(8,128)(2,1)S(1)}, u32[]{:S(2)}, u32[]{:S(2)}) collective-permute-start(bf16[256,640]{1,0:T(8,128)(2,1)} %get-tuple-element.75), channel_id=1, source_target_pairs={{0,20},{1,21},{4,16},{5,17},{16,4},{17,5},{20,0},{21,1},{2,22},{3,... | collective-permute-start | bytes 983048 | tf_op jit(solution)/shard_map/ppermute | solution.py:395
  239.2 28.4 %collective-permute-start.29 = (bf16[256,640]{1,0:T(8,128)(2,1)}, bf16[256,640]{1,0:T(8,128)(2,1)S(1)}, u32[]{:S(2)}, u32[]{:S(2)}) collective-permute-start(bf16[256,640]{1,0:T(8,128)(2,1)} %get-tuple-element.76), channel_id=1, source_target_pairs={{0,21},{1,20},{4,17},{5,16},{16,5},{17,4},{20,1},{21,0},{2,23},{3,... | collective-permute-start | bytes 983048 | tf_op jit(solution)/shard_map/ppermute | solution.py:395
  246.8 20.9 %collective-permute-start.23 = (bf16[256,640]{1,0:T(8,128)(2,1)}, bf16[256,640]{1,0:T(8,128)(2,1)S(1)}, u32[]{:S(2)}, u32[]{:S(2)}) collective-permute-start(bf16[256,640]{1,0:T(8,128)(2,1)} %get-tuple-element.70), channel_id=1, source_target_pairs={{0,1},{1,0},{4,5},{5,4},{16,17},{17,16},{20,21},{21,20},{2,3},{3,2... | collective-permute-start | bytes 983048 | tf_op jit(solution)/shard_map/ppermute | solution.py:395
  261.4 7.3 %collective-permute-start.24 = (bf16[256,640]{1,0:T(8,128)(2,1)}, bf16[256,640]{1,0:T(8,128)(2,1)S(1)}, u32[]{:S(2)}, u32[]{:S(2)}) collective-permute-start(bf16[256,640]{1,0:T(8,128)(2,1)} %get-tuple-element.71), channel_id=1, source_target_pairs={{0,4},{1,5},{4,0},{5,1},{16,20},{17,21},{20,16},{21,17},{2,6},{3,7... | collective-permute-start | bytes 983048 | tf_op jit(solution)/shard_map/ppermute | solution.py:395
  265.4 9.8 %collective-permute-start.25 = (bf16[256,640]{1,0:T(8,128)(2,1)}, bf16[256,640]{1,0:T(8,128)(2,1)S(1)}, u32[]{:S(2)}, u32[]{:S(2)}) collective-permute-start(bf16[256,640]{1,0:T(8,128)(2,1)} %get-tuple-element.72), channel_id=1, source_target_pairs={{0,5},{1,4},{4,1},{5,0},{16,21},{17,20},{20,17},{21,16},{2,7},{3,6... | collective-permute-start | bytes 983048 | tf_op jit(solution)/shard_map/ppermute | solution.py:395
  (17 other events, 340.7 us)

commit v4 on v3

--- a/solution.py
+++ b/solution.py
@@ -308,8 +308,9 @@
             o_ref[...] = (out * factor).astype(bf16)
 
 
-def outputs(ids, gated, weight, start, count, heads):
+def outputs(ids, gated, weight, bit, heads):
     tokens, width = gated.shape
+    low, count = heads // 4, heads // 2
     rows = tokens // heads
     return pl.pallas_call(
         output_kernel,
@@ -317,7 +318,7 @@
             num_scalar_prefetch=1,
             grid=(count,),
             in_specs=[
-                pl.BlockSpec((rows, width), lambda i, ids: (ids[2] ^ (start + i), 0)),
+                pl.BlockSpec((rows, width), lambda i, ids: (ids[2] ^ (i // low * 2 * low + bit * low + i % low), 0)),
                 pl.BlockSpec((width, width), lambda i, ids: (0, 0)),
             ],
             out_specs=[pl.BlockSpec((rows, width), lambda i, ids: (0, 0))] * count,
@@ -410,12 +411,13 @@
     new_third = updated(ids, full_third, w_third)
     gated = over_tokens(gate_kernel, query_local.reshape(-1, width), new_first, new_third)
     new_second = updated(ids, full_second, w_second)
-    far = heads // 2
-    blocks = outputs(ids, gated, new_second, far, heads - far, heads)
-    back = [swap(block, far + k) for k, block in enumerate(blocks)]
-    blocks = outputs(ids, gated, new_second, 0, far, heads)
-    near = [blocks[0]] + [swap(block, k) for k, block in enumerate(blocks) if k]
-    return back_to_columns(ids, near + back)
+    ready = [None] * heads
+    for bit in (1, 0):
+        blocks = outputs(ids, gated, new_second, bit, heads)
+        places = [k for k in range(heads) if (k // (heads // 4)) % 2 == bit]
+        for k, block in reversed(list(zip(places, blocks))):
+            ready[k] = swap(block, k) if k else block
+    return back_to_columns(ids, ready)
 
 
 def solution(mesh):

time: 282 us -> 284 us (level)
  transfers between devices with their start and end apart: 31 -> 31, of which waited for: 16 -> 18; matrix products, arithmetic and copies ran while one was open for 1% -> 1% of each run, Pallas kernels for 24% -> 24%
where the time goes in v4:
time: 284 us; the launch traced here: 283 us
  waiting for transfers between devices  136 us (48%)
  Pallas kernels  91.7 us (32%)
  starting transfers between devices  48 us (17%)
  local copies, waits for them, and re-layouts  3.68 us (1%)
  other arithmetic  3.57 us (1%)
    ppermute x21, waiting for transfers between devices, swap(): return lax.ppermute(block, ('head', 'l1', 'l2'), pairs)  85.8 us
    ppermute x6, waiting for transfers between devices, summed(): came = lax.ppermute(send, axis, pairs)  49.8 us
    pallas_call x2, Pallas kernels, grad_call(): pl.pallas_call(functools.partial(kernel, heads), grid_spec=pltpu.Prefetch...  27.1 us
    ppermute x21, starting transfers between devices, swap(): return lax.ppermute(block, ('head', 'l1', 'l2'), pairs)  27 us
    pallas_call x3, Pallas kernels, updated(): pl.pallas_call(newton_kernel, grid_spec=pltpu.PrefetchScalarGridSpec(num_...  25.7 us
    ppermute x6, starting transfers between devices, summed(): came = lax.ppermute(send, axis, pairs)  12.6 us
    pallas_call x2, Pallas kernels, outputs(): pl.pallas_call(output_kernel, grid_spec=pltpu.PrefetchScalarGridSpec(num_...  11.7 us
    pallas_call x2, Pallas kernels, prepared_pair(): pl.pallas_call(pair_kernel, grid_spec=pltpu.PrefetchScalarGridSpec(num_sc...  10.1 us
  transfers between devices with their start and end apart: 31, of which 18 were waited for; matrix products, arithmetic and copies ran while one was open for 1% of the time, Pallas kernels for 24%

profile of v4, /device:TPU:0, one launch (start us, length us, event | category | flops | bytes accessed | tf_op | source)
XLA Modules:
  0.0 282.8 jit_solution(6364056821286767897)
XLA Ops:
  2.0 6.5 %shard_map.93 = (bf16[2,192,640]{2,1,0:T(8,128)(2,1)}, bf16[2,192,640]{2,1,0:T(8,128)(2,1)}, bf16[2,192,640]{2,1,0:T(8,128)(2,1)}, bf16[2,192,640]{2,1,0:T(8,128...) custom-call(s32[3]{0:T(128)} %pad_add_fusion.ids, ...), custom_call_target="tpu_custom_call" | custom-call | flops 11796480 | bytes 7864320 | tf_op jit(solution)/shard_map/pallas_call | solution.py:85
  8.5 3.0 %collective-permute-start.10 = (bf16[2,192,640]{2,1,0:T(8,128)(2,1)}, bf16[2,192,640]{2,1,0:T(8,128)(2,1)S(1)}, u32[]{:S(2)}, u32[]{:S(2)}) collective-permute-start(bf16[2,192,640]{2,1,0:T(8,128)(2,1)} %get-tuple-element.53), channel_id=1, source_target_pairs={{0,16},{1,17},{4,20},{5,21},{16,0},{17,1},{20,4},{21,5},{2,18},{3,... | collective-permute-start | bytes 1474568 | tf_op jit(solution)/shard_map/ppermute | solution.py:396
  12.2 4.5 %shard_map.91 = bf16[8,256,640]{2,1,0:T(8,128)(2,1)} custom-call(bf16[256,5120]{1,0:T(8,128)(2,1)} %x_ref.1, f32[1,5120]{1,0:T(1,128)} %bitcast.9), custom_call_target="tpu_custom_call" | custom-call | flops 10485760 | bytes 5242880 | tf_op jit(solution)/shard_map/pallas_call | solution.py:66
  16.8 3.6 %all-to-all-start = ((bf16[8,256,640]{2,1,0:T(8,128)(2,1)}), bf16[8,256,640]{2,1,0:T(8,128)(2,1)S(1)}, u32[]{:S(2)}, u32[]{:S(2)}) async-start(bf16[8,256,640]{2,1,0:T(8,128)(2,1)} %shard_map.91), calls=%async_computation | async-start | bytes 5242880 | tf_op jit(solution)/shard_map/all_to_all | solution.py:404
  20.4 3.6 %shard_map.92 = (bf16[2,64,640]{2,1,0:T(8,128)(2,1)}, bf16[2,64,640]{2,1,0:T(8,128)(2,1)}, bf16[2,64,640]{2,1,0:T(8,128)(2,1)}, bf16[2,64,640]{2,1,0:T(8,128)(2,...) custom-call(s32[3]{0:T(128)} %pad_add_fusion.ids, ...), custom_call_target="tpu_custom_call" | custom-call | flops 3932160 | bytes 2621440 | tf_op jit(solution)/shard_map/pallas_call | solution.py:85
  28.6 27.5 %collective-permute-done.refs_1_ = bf16[2,64,640]{2,1,0:T(8,128)(2,1)S(1)} collective-permute-done((bf16[2,64,640]{2,1,0:T(8,128)(2,1)}, bf16[2,64,640]{2,1,0:T(8,128)(2,1)S(1)}, u32[]{:S(2)}, u32[]{:S(2)}) %collective-permute-start) | collective-permute-done | bytes 163872 | tf_op jit(solution)/shard_map/ppermute | solution.py:396
  56.5 3.7 %collective-permute-done.1.refs_2_ = bf16[2,64,640]{2,1,0:T(8,128)(2,1)S(1)} collective-permute-done((bf16[2,64,640]{2,1,0:T(8,128)(2,1)}, bf16[2,64,640]{2,1,0:T(8,128)(2,1)S(1)}, u32[]{:S(2)}, u32[]{:S(2)}) %collective-permute-start.1) | collective-permute-done | bytes 163872 | tf_op jit(solution)/shard_map/ppermute | solution.py:396
  64.3 6.7 %collective-permute-done.12.refs_6_ = bf16[2,192,640]{2,1,0:T(8,128)(2,1)S(1)} collective-permute-done((bf16[2,192,640]{2,1,0:T(8,128)(2,1)}, bf16[2,192,640]{2,1,0:T(8,128)(2,1)S(1)}, u32[]{:S(2)}, u32[]{:S(2)}) %collective-permute-start.12) | collective-permute-done | bytes 491552 | tf_op jit(solution)/shard_map/ppermute | solution.py:396
  72.6 8.2 %collective-permute-done.7.refs_1_ = bf16[2,192,640]{2,1,0:T(8,128)(2,1)} collective-permute-done((bf16[2,192,640]{2,1,0:T(8,128)(2,1)}, bf16[2,192,640]{2,1,0:T(8,128)(2,1)}, u32[]{:S(2)}, u32[]{:S(2)}) %collective-permute-start.7) | collective-permute-done | bytes 491552 | tf_op jit(solution)/shard_map/ppermute | solution.py:396
  82.4 9.6 %collective-permute-done.8.refs_2_ = bf16[2,192,640]{2,1,0:T(8,128)(2,1)} collective-permute-done((bf16[2,192,640]{2,1,0:T(8,128)(2,1)}, bf16[2,192,640]{2,1,0:T(8,128)(2,1)}, u32[]{:S(2)}, u32[]{:S(2)}) %collective-permute-start.8) | collective-permute-done | bytes 491552 | tf_op jit(solution)/shard_map/ppermute | solution.py:396
  93.2 4.1 %collective-permute-done.9.refs_3_ = bf16[2,192,640]{2,1,0:T(8,128)(2,1)} collective-permute-done((bf16[2,192,640]{2,1,0:T(8,128)(2,1)}, bf16[2,192,640]{2,1,0:T(8,128)(2,1)}, u32[]{:S(2)}, u32[]{:S(2)}) %collective-permute-start.9) | collective-permute-done | bytes 491552 | tf_op jit(solution)/shard_map/ppermute | solution.py:396
  98.2 17.1 %shard_map.94 = (f32[640,640]{1,0:T(8,128)}, f32[640,640]{1,0:T(8,128)}, f32[640,640]{1,0:T(8,128)}, bf16[640,640]{1,0:T(8,128)(2,1)}, bf16[640,640]{1,0:T(8,128)(2,1)}, /*index=5*/bf16[640,640]{1,0:T(8,128)(2,1)}) custom-call(s32[3]{0:T(128)} %pad_add_fusion.ids, bf16[2,192,640]{2,1,0:T(8,128)(2,1)} %get-tuple-element.49.refs_0_, ...), custom_call_target="tpu_custom_call" | custom-call | flops 7549747200 | bytes 3932160 | tf_op jit(solution)/shard_map/pallas_call | solution.py:224
  115.3 10.0 %shard_map.95 = (bf16[320,640]{1,0:T(8,128)(2,1)}, f32[320,640]{1,0:T(8,128)}, bf16[320,640]{1,0:T(8,128)(2,1)}, f32[320,640]{1,0:T(8,128)}, bf16[320,640]{1,0:T(8,128)(2,1)}, /*index=5*/f32[320,640]{1,0:T(8,128)}) custom-call(s32[3]{0:T(128)} %pad_add_fusion.ids, bf16[2,64,640]{2,1,0:T(8,128)(2,1)} %get-tuple-element.41.refs_0_, ...), custom_call_target="tpu_custom_call" | custom-call | flops 2516582400 | bytes 1310720 | tf_op jit(solution)/shard_map/pallas_call | solution.py:224
  129.3 8.7 %collective-permute-done.20 = bf16[320,640]{1,0:T(8,128)(2,1)S(1)} collective-permute-done((bf16[320,640]{1,0:T(8,128)(2,1)}, bf16[320,640]{1,0:T(8,128)(2,1)S(1)}, u32[]{:S(2)}, u32[]{:S(2)}) %collective-permute-start.20) | collective-permute-done | bytes 409632 | tf_op jit(solution)/shard_map/ppermute | solution.py:351
  142.2 4.6 %collective-permute-done.17 = bf16[320,640]{1,0:T(8,128)(2,1)S(1)} collective-permute-done((bf16[320,640]{1,0:T(8,128)(2,1)}, bf16[320,640]{1,0:T(8,128)(2,1)S(1)}, u32[]{:S(2)}, u32[]{:S(2)}) %collective-permute-start.17) | collective-permute-done | bytes 409632 | tf_op jit(solution)/shard_map/ppermute | solution.py:351
  151.0 3.7 %collective-permute-done.14 = bf16[320,640]{1,0:T(8,128)(2,1)S(1)} collective-permute-done((bf16[320,640]{1,0:T(8,128)(2,1)}, bf16[320,640]{1,0:T(8,128)(2,1)S(1)}, u32[]{:S(2)}, u32[]{:S(2)}) %collective-permute-start.14) | collective-permute-done | bytes 409632 | tf_op jit(solution)/shard_map/ppermute | solution.py:351
  157.7 19.8 %collective-permute-done.21 = bf16[320,640]{1,0:T(8,128)(2,1)S(1)} collective-permute-done((bf16[320,640]{1,0:T(8,128)(2,1)S(1)}, bf16[320,640]{1,0:T(8,128)(2,1)S(1)}, u32[]{:S(2)}, u32[]{:S(2)}) %collective-permute-start.21) | collective-permute-done | bytes 409632 | tf_op jit(solution)/shard_map/ppermute | solution.py:351
  179.2 7.1 %collective-permute-done.18 = bf16[320,640]{1,0:T(8,128)(2,1)S(1)} collective-permute-done((bf16[320,640]{1,0:T(8,128)(2,1)S(1)}, bf16[320,640]{1,0:T(8,128)(2,1)S(1)}, u32[]{:S(2)}, u32[]{:S(2)}) %collective-permute-start.18) | collective-permute-done | bytes 409632 | tf_op jit(solution)/shard_map/ppermute | solution.py:351
  187.9 6.0 %collective-permute-done.15 = bf16[320,640]{1,0:T(8,128)(2,1)S(1)} collective-permute-done((bf16[320,640]{1,0:T(8,128)(2,1)S(1)}, bf16[320,640]{1,0:T(8,128)(2,1)S(1)}, u32[]{:S(2)}, u32[]{:S(2)}) %collective-permute-start.15) | collective-permute-done | bytes 409632 | tf_op jit(solution)/shard_map/ppermute | solution.py:351
  195.7 8.5 %shard_map.99.u2_ref = bf16[640,640]{1,0:T(8,128)(2,1)} custom-call(s32[3]{0:T(128)} %pad_add_fusion.ids, bf16[320,640]{1,0:T(8,128)(2,1)} %copy-done.4, bf16[320,640]{1,0:T(8,128)(2,1)} %collective-permute-done.22.other_ref, f32[4,640,640]{2,1,0:T(8,128)} %w_ref.5), custom_call_target="tpu_custom_call" | custom-call | flops 3145728000 | bytes 3276800 | tf_op jit(solution)/shard_map/pallas_call | solution.py:280
  204.2 8.5 %shard_map.97.u3_ref = bf16[640,640]{1,0:T(8,128)(2,1)} custom-call(s32[3]{0:T(128)} %pad_add_fusion.ids, bf16[320,640]{1,0:T(8,128)(2,1)} %copy-done.5, bf16[320,640]{1,0:T(8,128)(2,1)} %collective-permute-done.19.other_ref, f32[4,640,640]{2,1,0:T(8,128)} %w_ref.4), custom_call_target="tpu_custom_call" | custom-call | flops 3145728000 | bytes 3276800 | tf_op jit(solution)/shard_map/pallas_call | solution.py:280
  212.7 8.7 %shard_map.96.u1_ref = bf16[640,640]{1,0:T(8,128)(2,1)} custom-call(s32[3]{0:T(128)} %pad_add_fusion.ids, bf16[320,640]{1,0:T(8,128)(2,1)} %copy-done.6, bf16[320,640]{1,0:T(8,128)(2,1)} %collective-permute-done.16.other_ref, f32[4,640,640]{2,1,0:T(8,128)} %w_ref.3), custom_call_target="tpu_custom_call" | custom-call | flops 3145728000 | bytes 3276800 | tf_op jit(solution)/shard_map/pallas_call | solution.py:280
  222.9 7.8 %shard_map.98.f_ref = bf16[2048,640]{1,0:T(8,128)(2,1)} custom-call(bf16[2048,640]{1,0:T(8,128)(2,1)} %bitcast.6, bf16[640,640]{1,0:T(8,128)(2,1)} %shard_map.96.u1_ref, bf16[640,640]{1,0:T(8,128)(2,1)} %shard_map.97.u3_ref), custom_call_target="tpu_custom_call" | custom-call | flops 3355443200 | bytes 5242880 | tf_op jit(solution)/shard_map/pallas_call | solution.py:337
  230.7 5.9 %shard_map.101 = (bf16[256,640]{1,0:T(8,128)(2,1)}, bf16[256,640]{1,0:T(8,128)(2,1)}, bf16[256,640]{1,0:T(8,128)(2,1)}, bf16[256,640]{1,0:T(8,128)(2,1)}) custom-call(s32[3]{0:T(128)} %pad_add_fusion.ids, bf16[2048,640]{1,0:T(8,128)(2,1)} %shard_map.98.f_ref, bf16[640,640]{1,0:T(8,128)(2,1)} %shard_map.99.u2_ref), custom_call_target="tpu_custom_call" | custom-call | flops 838860800 | bytes 2621440 | tf_op jit(solution)/shard_map/pallas_call | solution.py:315
  241.0 5.8 %shard_map.100 = (bf16[256,640]{1,0:T(8,128)(2,1)}, bf16[256,640]{1,0:T(8,128)(2,1)}, bf16[256,640]{1,0:T(8,128)(2,1)}, bf16[256,640]{1,0:T(8,128)(2,1)}) custom-call(s32[3]{0:T(128)} %pad_add_fusion.ids, bf16[2048,640]{1,0:T(8,128)(2,1)} %shard_map.98.f_ref, bf16[640,640]{1,0:T(8,128)(2,1)} %shard_map.99.u2_ref), custom_call_target="tpu_custom_call" | custom-call | flops 838860800 | bytes 2621440 | tf_op jit(solution)/shard_map/pallas_call | solution.py:315
  248.9 3.8 %collective-permute-done.25.refs_3_ = bf16[256,640]{1,0:T(8,128)(2,1)S(1)} collective-permute-done((bf16[256,640]{1,0:T(8,128)(2,1)}, bf16[256,640]{1,0:T(8,128)(2,1)S(1)}, u32[]{:S(2)}, u32[]{:S(2)}) %collective-permute-start.25) | collective-permute-done | bytes 327712 | tf_op jit(solution)/shard_map/ppermute | solution.py:396
  252.7 2.9 %collective-permute-start.27 = (bf16[256,640]{1,0:T(8,128)(2,1)}, bf16[256,640]{1,0:T(8,128)(2,1)S(1)}, u32[]{:S(2)}, u32[]{:S(2)}) collective-permute-start(bf16[256,640]{1,0:T(8,128)(2,1)} %get-tuple-element.74), channel_id=1, source_target_pairs={{0,17},{1,16},{4,21},{5,20},{16,1},{17,0},{20,5},{21,4},{2,19},{3,... | collective-permute-start | bytes 983048 | tf_op jit(solution)/shard_map/ppermute | solution.py:396
  255.6 6.8 %collective-permute-done.28.refs_6_ = bf16[256,640]{1,0:T(8,128)(2,1)S(1)} collective-permute-done((bf16[256,640]{1,0:T(8,128)(2,1)}, bf16[256,640]{1,0:T(8,128)(2,1)S(1)}, u32[]{:S(2)}, u32[]{:S(2)}) %collective-permute-start.28) | collective-permute-done | bytes 327712 | tf_op jit(solution)/shard_map/ppermute | solution.py:396
  262.5 3.1 %collective-permute-done.29.refs_7_ = bf16[256,640]{1,0:T(8,128)(2,1)S(1)} collective-permute-done((bf16[256,640]{1,0:T(8,128)(2,1)}, bf16[256,640]{1,0:T(8,128)(2,1)S(1)}, u32[]{:S(2)}, u32[]{:S(2)}) %collective-permute-start.29) | collective-permute-done | bytes 327712 | tf_op jit(solution)/shard_map/ppermute | solution.py:396
  265.6 6.7 %collective-permute-done.26.refs_4_ = bf16[256,640]{1,0:T(8,128)(2,1)S(1)} collective-permute-done((bf16[256,640]{1,0:T(8,128)(2,1)}, bf16[256,640]{1,0:T(8,128)(2,1)S(1)}, u32[]{:S(2)}, u32[]{:S(2)}) %collective-permute-start.26) | collective-permute-done | bytes 327712 | tf_op jit(solution)/shard_map/ppermute | solution.py:396
  272.2 5.1 %collective-permute-done.27.refs_5_ = bf16[256,640]{1,0:T(8,128)(2,1)S(1)} collective-permute-done((bf16[256,640]{1,0:T(8,128)(2,1)}, bf16[256,640]{1,0:T(8,128)(2,1)S(1)}, u32[]{:S(2)}, u32[]{:S(2)}) %collective-permute-start.27) | collective-permute-done | bytes 327712 | tf_op jit(solution)/shard_map/ppermute | solution.py:396
  278.1 4.7 %shard_map.102 = bf16[256,5120]{1,0:T(8,128)(2,1)} custom-call(s32[3]{0:T(128)} %pad_add_fusion.ids, bf16[256,640]{1,0:T(8,128)(2,1)} %get-tuple-element.69.refs_0_, bf16[256,640]{1,0:T(8,128)(2,1)} %copy-done.11, bf16[256,640]{1,0:T(8,128)(2,1)} %copy-done.7, bf16[256,640]{1,0:T(8,128)(2,1)} %copy-done.8, bf16[256,640]{1,0:T(8,128)(2,1)} %copy-done.12, ...), custom_call_target="tpu_custom_call" | custom-call | flops 1310720 | bytes 5242880 | tf_op jit(solution)/shard_map/pallas_call | solution.py:114
  (86 shorter events, 46.3 us)
Async XLA Ops:
  8.5 53.9 %collective-permute-start.10 = (bf16[2,192,640]{2,1,0:T(8,128)(2,1)}, bf16[2,192,640]{2,1,0:T(8,128)(2,1)S(1)}, u32[]{:S(2)}, u32[]{:S(2)}) collective-permute-start(bf16[2,192,640]{2,1,0:T(8,128)(2,1)} %get-tuple-element.53), channel_id=1, source_target_pairs={{0,16},{1,17},{4,20},{5,21},{16,0},{17,1},{20,4},{21,5},{2,18},{3,... | collective-permute-start | bytes 1474568 | tf_op jit(solution)/shard_map/ppermute | solution.py:396
  11.5 51.0 %collective-permute-start.11 = (bf16[2,192,640]{2,1,0:T(8,128)(2,1)}, bf16[2,192,640]{2,1,0:T(8,128)(2,1)}, u32[]{:S(2)}, u32[]{:S(2)}) collective-permute-start(bf16[2,192,640]{2,1,0:T(8,128)(2,1)} %get-tuple-element.54), channel_id=1, source_target_pairs={{0,5},{1,4},{4,1},{5,0},{16,21},{17,20},{20,17},{21,16},{2,7},{3,6... | collective-permute-start | bytes 1474568 | tf_op jit(solution)/shard_map/ppermute | solution.py:396
  16.8 204.6 %all-to-all-start = ((bf16[8,256,640]{2,1,0:T(8,128)(2,1)}), bf16[8,256,640]{2,1,0:T(8,128)(2,1)S(1)}, u32[]{:S(2)}, u32[]{:S(2)}) async-start(bf16[8,256,640]{2,1,0:T(8,128)(2,1)} %shard_map.91), calls=%async_computation | async-start | bytes 5242880 | tf_op jit(solution)/shard_map/all_to_all | solution.py:404
  24.0 32.1 %collective-permute-start = (bf16[2,64,640]{2,1,0:T(8,128)(2,1)}, bf16[2,64,640]{2,1,0:T(8,128)(2,1)S(1)}, u32[]{:S(2)}, u32[]{:S(2)}) collective-permute-start(bf16[2,64,640]{2,1,0:T(8,128)(2,1)} %get-tuple-element.42), channel_id=1, source_target_pairs={{0,21},{1,20},{4,17},{5,16},{16,5},{17,4},{20,1},{21,0},{2,23},{3,... | collective-permute-start | bytes 491528 | tf_op jit(solution)/shard_map/ppermute | solution.py:396
  26.6 33.6 %collective-permute-start.1 = (bf16[2,64,640]{2,1,0:T(8,128)(2,1)}, bf16[2,64,640]{2,1,0:T(8,128)(2,1)S(1)}, u32[]{:S(2)}, u32[]{:S(2)}) collective-permute-start(bf16[2,64,640]{2,1,0:T(8,128)(2,1)} %get-tuple-element.43), channel_id=1, source_target_pairs={{0,20},{1,21},{4,16},{5,17},{16,4},{17,5},{20,0},{21,1},{2,22},{3,... | collective-permute-start | bytes 491528 | tf_op jit(solution)/shard_map/ppermute | solution.py:396
  27.4 43.6 %collective-permute-start.12 = (bf16[2,192,640]{2,1,0:T(8,128)(2,1)}, bf16[2,192,640]{2,1,0:T(8,128)(2,1)S(1)}, u32[]{:S(2)}, u32[]{:S(2)}) collective-permute-start(bf16[2,192,640]{2,1,0:T(8,128)(2,1)} %get-tuple-element.55), channel_id=1, source_target_pairs={{0,4},{1,5},{4,0},{5,1},{16,20},{17,21},{20,16},{21,17},{2,6},{3,7... | collective-permute-start | bytes 1474568 | tf_op jit(solution)/shard_map/ppermute | solution.py:396
  56.1 59.2 %copy-start.16 = (bf16[2,64,640]{2,1,0:T(8,128)(2,1)}, bf16[2,64,640]{2,1,0:T(8,128)(2,1)S(1)}, u32[]{:S(2)}) copy-start(bf16[2,64,640]{2,1,0:T(8,128)(2,1)S(1)} %collective-permute-done.refs_1_) | copy-start | bytes 491524
  56.1 15.0 %collective-permute-start.13 = (bf16[2,192,640]{2,1,0:T(8,128)(2,1)}, bf16[2,192,640]{2,1,0:T(8,128)(2,1)}, u32[]{:S(2)}, u32[]{:S(2)}) collective-permute-start(bf16[2,192,640]{2,1,0:T(8,128)(2,1)} %get-tuple-element.56), channel_id=1, source_target_pairs={{0,1},{1,0},{4,5},{5,4},{16,17},{17,16},{20,21},{21,20},{2,3},{3,2... | collective-permute-start | bytes 1474568 | tf_op jit(solution)/shard_map/ppermute | solution.py:396
  60.2 20.7 %collective-permute-start.7 = (bf16[2,192,640]{2,1,0:T(8,128)(2,1)}, bf16[2,192,640]{2,1,0:T(8,128)(2,1)}, u32[]{:S(2)}, u32[]{:S(2)}) collective-permute-start(bf16[2,192,640]{2,1,0:T(8,128)(2,1)} %get-tuple-element.50), channel_id=1, source_target_pairs={{0,21},{1,20},{4,17},{5,16},{16,5},{17,4},{20,1},{21,0},{2,23},{3,... | collective-permute-start | bytes 1474568 | tf_op jit(solution)/shard_map/ppermute | solution.py:396
  62.3 29.6 %collective-permute-start.8 = (bf16[2,192,640]{2,1,0:T(8,128)(2,1)}, bf16[2,192,640]{2,1,0:T(8,128)(2,1)}, u32[]{:S(2)}, u32[]{:S(2)}) collective-permute-start(bf16[2,192,640]{2,1,0:T(8,128)(2,1)} %get-tuple-element.51), channel_id=1, source_target_pairs={{0,20},{1,21},{4,16},{5,17},{16,4},{17,5},{20,0},{21,1},{2,22},{3,... | collective-permute-start | bytes 1474568 | tf_op jit(solution)/shard_map/ppermute | solution.py:396
  62.5 34.9 %collective-permute-start.9 = (bf16[2,192,640]{2,1,0:T(8,128)(2,1)}, bf16[2,192,640]{2,1,0:T(8,128)(2,1)}, u32[]{:S(2)}, u32[]{:S(2)}) collective-permute-start(bf16[2,192,640]{2,1,0:T(8,128)(2,1)} %get-tuple-element.52), channel_id=1, source_target_pairs={{0,17},{1,16},{4,21},{5,20},{16,1},{17,0},{20,5},{21,4},{2,19},{3,... | collective-permute-start | bytes 1474568 | tf_op jit(solution)/shard_map/ppermute | solution.py:396
  71.0 44.3 %collective-permute-start.2 = (bf16[2,64,640]{2,1,0:T(8,128)(2,1)}, bf16[2,64,640]{2,1,0:T(8,128)(2,1)}, u32[]{:S(2)}, u32[]{:S(2)}) collective-permute-start(bf16[2,64,640]{2,1,0:T(8,128)(2,1)} %get-tuple-element.44), channel_id=1, source_target_pairs={{0,17},{1,16},{4,21},{5,20},{16,1},{17,0},{20,5},{21,4},{2,19},{3,... | collective-permute-start | bytes 491528 | tf_op jit(solution)/shard_map/ppermute | solution.py:396
  71.0 44.3 %collective-permute-start.3 = (bf16[2,64,640]{2,1,0:T(8,128)(2,1)}, bf16[2,64,640]{2,1,0:T(8,128)(2,1)}, u32[]{:S(2)}, u32[]{:S(2)}) collective-permute-start(bf16[2,64,640]{2,1,0:T(8,128)(2,1)} %get-tuple-element.45), channel_id=1, source_target_pairs={{0,16},{1,17},{4,20},{5,21},{16,0},{17,1},{20,4},{21,5},{2,18},{3,... | collective-permute-start | bytes 491528 | tf_op jit(solution)/shard_map/ppermute | solution.py:396
  80.9 34.5 %collective-permute-start.4 = (bf16[2,64,640]{2,1,0:T(8,128)(2,1)}, bf16[2,64,640]{2,1,0:T(8,128)(2,1)}, u32[]{:S(2)}, u32[]{:S(2)}) collective-permute-start(bf16[2,64,640]{2,1,0:T(8,128)(2,1)} %get-tuple-element.46), channel_id=1, source_target_pairs={{0,5},{1,4},{4,1},{5,0},{16,21},{17,20},{20,17},{21,16},{2,7},{3,6... | collective-permute-start | bytes 491528 | tf_op jit(solution)/shard_map/ppermute | solution.py:396
  91.9 23.4 %collective-permute-start.5 = (bf16[2,64,640]{2,1,0:T(8,128)(2,1)}, bf16[2,64,640]{2,1,0:T(8,128)(2,1)}, u32[]{:S(2)}, u32[]{:S(2)}) collective-permute-start(bf16[2,64,640]{2,1,0:T(8,128)(2,1)} %get-tuple-element.47), channel_id=1, source_target_pairs={{0,4},{1,5},{4,0},{5,1},{16,20},{17,21},{20,16},{21,17},{2,6},{3,7... | collective-permute-start | bytes 491528 | tf_op jit(solution)/shard_map/ppermute | solution.py:396
  97.3 18.0 %collective-permute-start.6 = (bf16[2,64,640]{2,1,0:T(8,128)(2,1)}, bf16[2,64,640]{2,1,0:T(8,128)(2,1)}, u32[]{:S(2)}, u32[]{:S(2)}) collective-permute-start(bf16[2,64,640]{2,1,0:T(8,128)(2,1)} %get-tuple-element.48), channel_id=1, source_target_pairs={{0,1},{1,0},{4,5},{5,4},{16,17},{17,16},{20,21},{21,20},{2,3},{3,2... | collective-permute-start | bytes 491528 | tf_op jit(solution)/shard_map/ppermute | solution.py:396
  125.4 12.6 %collective-permute-start.20 = (bf16[320,640]{1,0:T(8,128)(2,1)}, bf16[320,640]{1,0:T(8,128)(2,1)S(1)}, u32[]{:S(2)}, u32[]{:S(2)}) collective-permute-start(bf16[320,640]{1,0:T(8,128)(2,1)} %get-tuple-element.68), channel_id=1, source_target_pairs={{0,2},{2,0},{1,3},{3,1},{4,6},{6,4},{5,7},{7,5},{8,10},{10,8},{9,1... | collective-permute-start | bytes 1228808 | tf_op jit(solution)/shard_map/ppermute | solution.py:351
  127.3 19.5 %collective-permute-start.17 = (bf16[320,640]{1,0:T(8,128)(2,1)}, bf16[320,640]{1,0:T(8,128)(2,1)S(1)}, u32[]{:S(2)}, u32[]{:S(2)}) collective-permute-start(bf16[320,640]{1,0:T(8,128)(2,1)} %get-tuple-element.66), channel_id=1, source_target_pairs={{0,2},{2,0},{1,3},{3,1},{4,6},{6,4},{5,7},{7,5},{8,10},{10,8},{9,1... | collective-permute-start | bytes 1228808 | tf_op jit(solution)/shard_map/ppermute | solution.py:351
  127.5 27.2 %collective-permute-start.14 = (bf16[320,640]{1,0:T(8,128)(2,1)}, bf16[320,640]{1,0:T(8,128)(2,1)S(1)}, u32[]{:S(2)}, u32[]{:S(2)}) collective-permute-start(bf16[320,640]{1,0:T(8,128)(2,1)} %get-tuple-element.64), channel_id=1, source_target_pairs={{0,2},{2,0},{1,3},{3,1},{4,6},{6,4},{5,7},{7,5},{8,10},{10,8},{9,1... | collective-permute-start | bytes 1228808 | tf_op jit(solution)/shard_map/ppermute | solution.py:351
  139.3 38.2 %collective-permute-start.21 = (bf16[320,640]{1,0:T(8,128)(2,1)S(1)}, bf16[320,640]{1,0:T(8,128)(2,1)S(1)}, u32[]{:S(2)}, u32[]{:S(2)}) collective-permute-start(bf16[320,640]{1,0:T(8,128)(2,1)S(1)} %fusion.2), channel_id=1, source_target_pairs={{0,8},{8,0},{1,9},{9,1},{2,10},{10,2},{3,11},{11,3},{4,12},{12,4},... | collective-permute-start | bytes 1228808 | tf_op jit(solution)/shard_map/ppermute | solution.py:351
  148.1 38.1 %collective-permute-start.18 = (bf16[320,640]{1,0:T(8,128)(2,1)S(1)}, bf16[320,640]{1,0:T(8,128)(2,1)S(1)}, u32[]{:S(2)}, u32[]{:S(2)}) collective-permute-start(bf16[320,640]{1,0:T(8,128)(2,1)S(1)} %fusion.1), channel_id=1, source_target_pairs={{0,8},{8,0},{1,9},{9,1},{2,10},{10,2},{3,11},{11,3},{4,12},{12,4},... | collective-permute-start | bytes 1228808 | tf_op jit(solution)/shard_map/ppermute | solution.py:351
  154.8 39.1 %collective-permute-start.15 = (bf16[320,640]{1,0:T(8,128)(2,1)S(1)}, bf16[320,640]{1,0:T(8,128)(2,1)S(1)}, u32[]{:S(2)}, u32[]{:S(2)}) collective-permute-start(bf16[320,640]{1,0:T(8,128)(2,1)S(1)} %fusion), channel_id=1, source_target_pairs={{0,8},{8,0},{1,9},{9,1},{2,10},{10,2},{3,11},{11,3},{4,12},{12,4},... | collective-permute-start | bytes 1228808 | tf_op jit(solution)/shard_map/ppermute | solution.py:351
  177.6 18.1 %collective-permute-start.22 = (bf16[320,640]{1,0:T(8,128)(2,1)S(1)}, bf16[320,640]{1,0:T(8,128)(2,1)}, u32[]{:S(2)}, u32[]{:S(2)}) collective-permute-start(bf16[320,640]{1,0:T(8,128)(2,1)S(1)} %add_convert_fusion.own_ref), channel_id=1, source_target_pairs={{0,2},{2,0},{1,3},{3,1},{4,6},{6,4},{5,7},{7,5},{8,10},{10,8},{9,1... | collective-permute-start | bytes 1228808 | tf_op jit(solution)/shard_map/ppermute | solution.py:365
  186.3 17.9 %collective-permute-start.19 = (bf16[320,640]{1,0:T(8,128)(2,1)S(1)}, bf16[320,640]{1,0:T(8,128)(2,1)}, u32[]{:S(2)}, u32[]{:S(2)}) collective-permute-start(bf16[320,640]{1,0:T(8,128)(2,1)S(1)} %add_convert_fusion.1.own_ref), channel_id=1, source_target_pairs={{0,2},{2,0},{1,3},{3,1},{4,6},{6,4},{5,7},{7,5},{8,10},{10,8},{9,1... | collective-permute-start | bytes 1228808 | tf_op jit(solution)/shard_map/ppermute | solution.py:365
  194.1 18.6 %collective-permute-start.16 = (bf16[320,640]{1,0:T(8,128)(2,1)S(1)}, bf16[320,640]{1,0:T(8,128)(2,1)}, u32[]{:S(2)}, u32[]{:S(2)}) collective-permute-start(bf16[320,640]{1,0:T(8,128)(2,1)S(1)} %add_convert_fusion.2.own_ref), channel_id=1, source_target_pairs={{0,2},{2,0},{1,3},{3,1},{4,6},{6,4},{5,7},{7,5},{8,10},{10,8},{9,1... | collective-permute-start | bytes 1228808 | tf_op jit(solution)/shard_map/ppermute | solution.py:365
  236.6 10.8 %collective-permute-start.24 = (bf16[256,640]{1,0:T(8,128)(2,1)}, bf16[256,640]{1,0:T(8,128)(2,1)S(1)}, u32[]{:S(2)}, u32[]{:S(2)}) collective-permute-start(bf16[256,640]{1,0:T(8,128)(2,1)} %get-tuple-element.71), channel_id=1, source_target_pairs={{0,4},{1,5},{4,0},{5,1},{16,20},{17,21},{20,16},{21,17},{2,6},{3,7... | collective-permute-start | bytes 983048 | tf_op jit(solution)/shard_map/ppermute | solution.py:396
  237.3 15.4 %collective-permute-start.25 = (bf16[256,640]{1,0:T(8,128)(2,1)}, bf16[256,640]{1,0:T(8,128)(2,1)S(1)}, u32[]{:S(2)}, u32[]{:S(2)}) collective-permute-start(bf16[256,640]{1,0:T(8,128)(2,1)} %get-tuple-element.72), channel_id=1, source_target_pairs={{0,5},{1,4},{4,1},{5,0},{16,21},{17,20},{20,17},{21,16},{2,7},{3,6... | collective-permute-start | bytes 983048 | tf_op jit(solution)/shard_map/ppermute | solution.py:396
  237.3 25.2 %collective-permute-start.28 = (bf16[256,640]{1,0:T(8,128)(2,1)}, bf16[256,640]{1,0:T(8,128)(2,1)S(1)}, u32[]{:S(2)}, u32[]{:S(2)}) collective-permute-start(bf16[256,640]{1,0:T(8,128)(2,1)} %get-tuple-element.75), channel_id=1, source_target_pairs={{0,20},{1,21},{4,16},{5,17},{16,4},{17,5},{20,0},{21,1},{2,22},{3,... | collective-permute-start | bytes 983048 | tf_op jit(solution)/shard_map/ppermute | solution.py:396
  239.6 26.0 %collective-permute-start.29 = (bf16[256,640]{1,0:T(8,128)(2,1)}, bf16[256,640]{1,0:T(8,128)(2,1)S(1)}, u32[]{:S(2)}, u32[]{:S(2)}) collective-permute-start(bf16[256,640]{1,0:T(8,128)(2,1)} %get-tuple-element.76), channel_id=1, source_target_pairs={{0,21},{1,20},{4,17},{5,16},{16,5},{17,4},{20,1},{21,0},{2,23},{3,... | collective-permute-start | bytes 983048 | tf_op jit(solution)/shard_map/ppermute | solution.py:396
  246.8 18.7 %collective-permute-start.23 = (bf16[256,640]{1,0:T(8,128)(2,1)}, bf16[256,640]{1,0:T(8,128)(2,1)S(1)}, u32[]{:S(2)}, u32[]{:S(2)}) collective-permute-start(bf16[256,640]{1,0:T(8,128)(2,1)} %get-tuple-element.70), channel_id=1, source_target_pairs={{0,1},{1,0},{4,5},{5,4},{16,17},{17,16},{20,21},{21,20},{2,3},{3,2... | collective-permute-start | bytes 983048 | tf_op jit(solution)/shard_map/ppermute | solution.py:396
  247.4 24.8 %collective-permute-start.26 = (bf16[256,640]{1,0:T(8,128)(2,1)}, bf16[256,640]{1,0:T(8,128)(2,1)S(1)}, u32[]{:S(2)}, u32[]{:S(2)}) collective-permute-start(bf16[256,640]{1,0:T(8,128)(2,1)} %get-tuple-element.73), channel_id=1, source_target_pairs={{0,16},{1,17},{4,20},{5,21},{16,0},{17,1},{20,4},{21,5},{2,18},{3,... | collective-permute-start | bytes 983048 | tf_op jit(solution)/shard_map/ppermute | solution.py:396
  252.7 24.6 %collective-permute-start.27 = (bf16[256,640]{1,0:T(8,128)(2,1)}, bf16[256,640]{1,0:T(8,128)(2,1)S(1)}, u32[]{:S(2)}, u32[]{:S(2)}) collective-permute-start(bf16[256,640]{1,0:T(8,128)(2,1)} %get-tuple-element.74), channel_id=1, source_target_pairs={{0,17},{1,16},{4,21},{5,20},{16,1},{17,0},{20,5},{21,4},{2,19},{3,... | collective-permute-start | bytes 983048 | tf_op jit(solution)/shard_map/ppermute | solution.py:396
  (17 other events, 385.4 us)
